TPU v7x, 128 devices: a whole 4x4x4 slice. The times are simulated.
128 devices in a mesh: gx: 4 (over z_lo, core), gy: 16 (over x, y), gz: 2 (over z_hi).
Axes of the slice: x: 4, y: 4, z: 4 (z_hi: 2, z_lo: 2; z = z_hi * 2 + z_lo), core: 2. Of those that a mesh axis runs over, the one named last changes fastest.
Arguments:
- eigvecs: bfloat16 [64, 128, 96, 512], P('gx', 'gy', 'gz'), may hold values from -7 to 7, as said below
- material: float32 [2, 64, 128, 96], P(None, 'gx', 'gy', 'gz'), may hold values from 0.5 to 2
Outputs:
- stiffness: float32 [512, 512], P(('gx', 'gy', 'gz'))
- mass_matrix: float32 [512, 512], P(('gx', 'gy', 'gz'))
Inputs may be any that keep to these rules, and one draw needn't show every extreme that they name: `eigvecs`: entries are a rough part plus a part that varies slowly over the grid.
All inputs are finite; a program needn't handle non-finite values.
Results may differ from a plain program's by a relative error of at most 0.0003.
Values may be sent and summed in bfloat16 or wider, within the bound.
A program may use at most 128 MiB of HBM per device.

v0:
```python
import jax
import jax.numpy as jnp
from jax import lax
from jax.sharding import PartitionSpec as P

corner_weight = 0.0625
coupling_total = 3.5
mass_side = 1.0 / 6.0
mass_middle = 4.0 / 6.0


def with_halo(cells, sides, width):
    for axis, dim in sides:
        count = lax.axis_size(axis)
        ends = count - 1
        head = lax.slice_in_dim(cells, 0, width, axis=dim)
        tail = lax.slice_in_dim(cells, cells.shape[dim] - width, cells.shape[dim], axis=dim)
        cells = jnp.concatenate(
            [
                lax.ppermute(tail, axis, [(i, (i + 1) % count) for i in range(ends)]),
                cells,
                lax.ppermute(head, axis, [((i + 1) % count, i) for i in range(ends)]),
            ],
            axis=dim,
        )
    return cells


def split_up(x, dim, devices):
    dims = x.shape
    parts = x.reshape(*dims[:dim], devices, dims[dim] // devices, *dims[dim + 1 :])
    return jnp.moveaxis(parts, dim, 0)


def sum_at_owner(x, axis, dim):
    devices = lax.axis_size(axis)
    parts = lax.all_to_all(split_up(x, dim, devices), axis, 0, 0, tiled=True)
    return jnp.sum(parts, axis=0)


def three_taps(field, side, middle):
    for axis_dim in (0, 1, 2):
        inner = field.shape[axis_dim] - 2
        lower = lax.slice_in_dim(field, 0, inner, axis=axis_dim)
        centre = lax.slice_in_dim(field, 1, inner + 1, axis=axis_dim)
        upper = lax.slice_in_dim(field, 2, inner + 2, axis=axis_dim)
        field = side * (lower + upper) + middle * centre
    return field


def apply_operators(padded, padded_material):
    values = padded.astype(jnp.float32)
    kappa = padded_material[0]
    rho = padded_material[1]
    centre = values[1:-1, 1:-1, 1:-1]
    kappa_centre = kappa[1:-1, 1:-1, 1:-1]
    rho_centre = rho[1:-1, 1:-1, 1:-1]
    kappa_values = kappa[..., None] * values
    rho_values = rho[..., None] * values
    self_weight = 8.0 * corner_weight
    near_values = corner_weight * three_taps(values, 1.0, 2.0) - self_weight * centre
    near_kappa_values = (
        corner_weight * three_taps(kappa_values, 1.0, 2.0)
        - self_weight * kappa_values[1:-1, 1:-1, 1:-1]
    )
    near_kappa = corner_weight * three_taps(kappa, 1.0, 2.0) - self_weight * kappa_centre
    row_weight = 0.5 * (coupling_total * kappa_centre + near_kappa)
    stiff_sum = (
        row_weight[..., None] * centre
        - 0.5 * kappa_centre[..., None] * near_values
        - 0.5 * near_kappa_values
    )
    mass_sum = 0.5 * rho_centre[..., None] * three_taps(
        values, mass_side, mass_middle
    ) + 0.5 * three_taps(rho_values, mass_side, mass_middle)
    return (stiff_sum.astype(jnp.bfloat16), mass_sum.astype(jnp.bfloat16))


def per_device(eigvecs, material):
    size_x, size_y, size_z, columns = eigvecs.shape
    cells = size_x * size_y * size_z
    block_cols = 128
    padded_material = with_halo(material, (("gx", 1), ("gy", 2), ("gz", 3)), 1)
    padded = with_halo(eigvecs, (("gx", 0), ("gy", 1), ("gz", 2)), 1)

    def column_block(block_index):
        col_block = lax.dynamic_slice_in_dim(padded, block_index * block_cols, block_cols, 3)
        stiff_vecs, mass_vecs = apply_operators(col_block, padded_material)
        return (stiff_vecs.reshape(cells, block_cols), mass_vecs.reshape(cells, block_cols))

    stiff_blocks, mass_blocks = lax.map(
        column_block, jnp.arange(columns // block_cols, dtype=jnp.int32)
    )
    flat_vectors = eigvecs.reshape(cells, columns)
    devices_all = lax.axis_size("gx") * lax.axis_size("gy") * lax.axis_size("gz")
    total_cells = cells * devices_all
    row_count = columns // lax.axis_size("gx") * lax.axis_size("gx")
    stiff_part = jnp.einsum(
        "cp,bcq->pbq", flat_vectors, stiff_blocks, preferred_element_type=jnp.float32
    ).reshape(row_count, columns)
    mass_part = jnp.einsum(
        "cp,bcq->pbq", flat_vectors, mass_blocks, preferred_element_type=jnp.float32
    ).reshape(row_count, columns)
    section_one = sum_at_owner(jnp.concatenate([stiff_part, mass_part], axis=1), "gx", 0)
    section_two = sum_at_owner(section_one, "gy", 0)
    summed = sum_at_owner(section_two, "gz", 0)
    stiffness = summed[:, :columns] / total_cells
    mass_matrix = summed[:, columns:] / total_cells
    return (stiffness, mass_matrix)


def solution(mesh):
    return jax.shard_map(
        per_device,
        mesh=mesh,
        in_specs=(P("gx", "gy", "gz", None), P(None, "gx", "gy", "gz")),
        out_specs=(P(("gx", "gy", "gz"), None), P(("gx", "gy", "gz"), None)),
        check_vma=False,
    )
```

profile of v0, /device:TPU:0, one launch (start us, length us, event | category | flops | bytes accessed | tf_op | source)
XLA Modules:
  0.0 277.3 jit_solution(3379979988916823563)
XLA Ops:
  0.6 1.2 fusion.36
  1.8 1.3 collective-permute-start.6
  3.1 0.7 fusion.39
  3.8 4.6 %collective-permute-start = (f32[2,1,8,48]{3,2,1,0:T(8,128)S(1)}, f32[2,1,8,48]{3,2,1,0:T(8,128)S(1)}, u32[]{:S(2)}, u32[]{:S(2)}) collective-permute-start(f32[2,1,8,48]{3,2,1,0:T(8,128)S(1)} %get-tuple-element.101), channel_id=1, source_target_pairs={{0,32},{32,64},{64,96},{1,33},{33,65},{65,97},{2,34},{34,66},{66,9... | collective-permute-start | bytes 9224 | tf_op jit(solution)/shard_map/ppermute | solution.py:20
  8.5 1.3 collective-permute-start.1
  9.8 1.3 collective-permute-start.7
  11.2 3.9 %constant_dynamic-update-slice_fusion.6 = bf16[18,8,48,512]{3,2,1,0:T(8,128)(2,1)S(1)} fusion(bf16[18,8,48,512]{3,2,1,0:T(8,128)(2,1)S(1)} %constant_dynamic-update-slice_fusion.7, bf16[16,8,48,512]{3,2,1,0:T(8,128)(2,1)} %param.4), kind=kLoop, calls=%fused_computation.87 | loop fusion | bytes 12582912
  15.1 2.9 %copy-done.1 = bf16[18,8,48,512]{3,2,1,0:T(8,128)(2,1)} copy-done((bf16[18,8,48,512]{3,2,1,0:T(8,128)(2,1)}, bf16[18,8,48,512]{3,2,1,0:T(8,128)(2,1)S(1)}, u32[]{:S(2)}) %copy-start.1) | copy-done | bytes 7077912
  17.9 1.4 fusion.35
  19.4 1.3 collective-permute-start.9
  20.7 5.5 %collective-permute-start.8 = (bf16[18,1,48,512]{3,2,1,0:T(8,128)(2,1)}, bf16[18,1,48,512]{3,2,1,0:T(8,128)(2,1)}, u32[]{:S(2)}, u32[]{:S(2)}) collective-permute-start(bf16[18,1,48,512]{3,2,1,0:T(8,128)(2,1)} %get-tuple-element.92), channel_id=1, source_target_pairs={{0,2},{2,4},{4,6},{6,8},{8,10},{10,12},{12,14},{14,16},{16,18},{18... | collective-permute-start | bytes 2654216 | tf_op jit(solution)/shard_map/ppermute | solution.py:20
  26.2 1.6 collective-permute-start.3
  27.8 4.5 %collective-permute-start.2 = (f32[2,18,1,48]{3,2,1,0:T(1,128)S(1)}, f32[2,18,1,48]{3,2,1,0:T(1,128)S(1)}, u32[]{:S(2)}, u32[]{:S(2)}) collective-permute-start(f32[2,18,1,48]{3,2,1,0:T(1,128)S(1)} %get-tuple-element.98), channel_id=1, source_target_pairs={{0,2},{2,4},{4,6},{6,8},{8,10},{10,12},{12,14},{14,16},{16,18},{18... | collective-permute-start | bytes 20744 | tf_op jit(solution)/shard_map/ppermute | solution.py:20
  32.3 8.1 %collective-permute-done.3 = f32[2,18,1,48]{3,2,1,0:T(1,128)S(1)} collective-permute-done((f32[2,18,1,48]{3,2,1,0:T(1,128)S(1)}, f32[2,18,1,48]{3,2,1,0:T(1,128)S(1)}, u32[]{:S(2)}, u32[]{:S(2)}) %collective-permute-start.3) | collective-permute-done | bytes 6944 | tf_op jit(solution)/shard_map/ppermute | solution.py:22
  40.4 1.7 collective-permute-done.2
  42.2 1.0 fusion.37
  43.2 1.3 collective-permute-start.5
  44.5 6.8 %collective-permute-start.4 = (f32[2,18,10,1]{3,2,1,0:T(8,128)}, f32[2,18,10,1]{3,2,1,0:T(8,128)}, u32[]{:S(2)}, u32[]{:S(2)}) collective-permute-start(f32[2,18,10,1]{3,2,1,0:T(8,128)} %get-tuple-element.96), channel_id=1, source_target_pairs={{0,1},{2,3},{4,5},{6,7},{8,9},{10,11},{12,13},{14,15},{16,17},{18,... | collective-permute-start | bytes 4328 | tf_op jit(solution)/shard_map/ppermute | solution.py:20
  51.2 2.5 collective-permute-done.5
  53.8 0.7 copy-done.2
  54.5 1.1 collective-permute-done.4
  55.6 1.3 pad_maximum_fusion.6
  57.0 2.6 pad_maximum_fusion.4
  59.6 1.3 collective-permute-start.11
  60.9 6.3 %collective-permute-start.10 = (bf16[18,10,1,512]{3,2,1,0:T(2,128)(2,1)S(1)}, bf16[18,10,1,512]{3,2,1,0:T(2,128)(2,1)S(1)}, u32[]{:S(2)}, u32[]{:S(2)}) collective-permute-start(bf16[18,10,1,512]{3,2,1,0:T(2,128)(2,1)S(1)} %get-tuple-element.90), channel_id=1, source_target_pairs={{0,1},{2,3},{4,5},{6,7},{8,9},{10,11},{12,13},{14,15},{16,17},{18,... | collective-permute-start | bytes 552968 | tf_op jit(solution)/shard_map/ppermute | solution.py:20
  67.2 5.5 %collective-permute-done.11 = bf16[18,10,1,512]{3,2,1,0:T(2,128)(2,1)S(1)} collective-permute-done((bf16[18,10,1,512]{3,2,1,0:T(2,128)(2,1)S(1)}, bf16[18,10,1,512]{3,2,1,0:T(2,128)(2,1)S(1)}, u32[]{:S(2)}, u32[]{:S(2)}) %collective-permute-start.11) | collective-permute-done | bytes 184352 | tf_op jit(solution)/shard_map/ppermute | solution.py:22
  72.7 1.8 collective-permute-done.10
  74.5 9.4 %pad_maximum_fusion = bf16[18,10,50,512]{3,2,1,0:T(8,128)(2,1)} fusion(bf16[18,10,1,512]{3,2,1,0:T(2,128)(2,1)S(1)} %collective-permute-done.11, bf16[18,1,48,512]{3,2,1,0:T(8,128)(2,1)} %collective-permute-done.9, bf16[18,8,48,512]{3,2,1,0:T(8,128)(2,1)S(1)} %bitcast.42, bf16[18,1,48,512]{3,2,1,0:T(8,128)(2,1)} %collective-permute-done.8, ...), kind=kLoop, calls=%fused_computation.72 | loop fusion | flops 46080000 | bytes 18432000 | tf_op jit(solution)/shard_map/concatenate | solution.py:18
  83.9 114.4 %while.13 = (s32[]{:T(128)}, bf16[4,6144,128]{2,1,0:T(8,128)(2,1)}, bf16[4,6144,128]{2,1,0:T(8,128)(2,1)}, f32[2,18,10,50]{3,2,1,0:T(8,128)S(1)}, f32[16,10,50]{...) while((s32[]{:T(128)}, bf16[4,6144,128]{2,1,0:T(8,128)(2,1)}, ...), condition=%wide.region_1.2_spmd, body=%wide.region_0.1_spmd.sunk | while | flops 53078404 | bytes 184562576 | solution.py:91
  85.2 5.8 %broadcast_multiply_fusion.3 = (f32[18,10,50,128]{3,2,1,0:T(8,128)S(1)}, f32[18,10,50,128]{3,2,1,0:T(8,128)S(1)}) fusion(f32[18,10,50]{2,1,0:T(8,128)S(1)} %get-tuple-element.157, bf16[18,10,50,512]{3,2,1,0:T(8,128)(2,1)} %get-tuple-element.195, s32[]{:T(128)S(6)} %select_n.5, f32[18,10,50]{2,1,0:T(8,128)S(1)} %get-tuple-element.158), kind=kLoop, calls=%fused_computation.52.clone.1 | loop fusion | flops 3456000 | bytes 11592004 | tf_op jit(solution)/shard_map/while/body/eval_jaxpr/mul | solution.py:59
  91.0 0.6 fusion.54
  92.1 2.1 dynamic-slice_convert_fusion.2
  94.2 2.9 %multiply_add_fusion.3 = (f32[16,10,50,128]{3,2,1,0:T(8,128)S(1)}, f32[16,10,50,128]{3,2,1,0:T(8,128)}) fusion(f32[18,10,50,128]{3,2,1,0:T(8,128)S(1)} %dynamic-slice_convert_fusion.2), kind=kLoop, calls=%fused_computation.8.clone.1 | loop fusion | flops 6144000 | bytes 20480000 | tf_op jit(solution)/shard_map/while/body/eval_jaxpr/add | solution.py:47
  97.6 3.1 %fusion.57 = bf16[16,8,48,128]{3,2,1,0:T(8,128)(2,1)} fusion(f32[16,8,50,128]{3,2,1,0:T(8,128)S(1)} %fusion.55, f32[16,8,50,128]{3,2,1,0:T(8,128)S(1)} %fusion.56, f32[16,8,48]{2,1,0:T(8,128)S(1)} %slice_multiply_fusion.18), kind=kLoop, calls=%fused_computation.28.clone.1 | loop fusion | flops 9437184 | bytes 20471808 | tf_op jit(solution)/shard_map/while/body/eval_jaxpr/convert_element_type | solution.py:76
  101.7 5.2 %fusion.60 = f32[16,8,50,128]{3,2,1,0:T(8,128)S(1)} fusion(f32[16,10,50,128]{3,2,1,0:T(8,128)} %get-tuple-element.162), kind=kLoop, calls=%fused_computation.22.clone.1 | loop fusion | flops 2457600 | bytes 13107200 | tf_op jit(solution)/shard_map/while/body/eval_jaxpr/add | solution.py:47
  107.1 3.6 %fusion.63 = bf16[16,8,48,128]{3,2,1,0:T(8,128)(2,1)S(1)} fusion(f32[18,10,50,128]{3,2,1,0:T(8,128)S(1)} %get-tuple-element.161, f32[16,8,50,128]{3,2,1,0:T(8,128)S(1)} %fusion.59, f32[16,8,50,128]{3,2,1,0:T(8,128)S(1)} %fusion.60, f32[18,10,50,128]{3,2,1,0:T(8,128)S(1)} %dynamic-slice_convert_fusion.2, f32[16,8,48]{2,1,0:T(8,128)S(1)} %get-tuple-element.163, ...), kind=kLoop, calls=%fused_computation.40.clone.1 | loop fusion | flops 14155776 | bytes 26787840 | tf_op jit(solution)/shard_map/while/body/eval_jaxpr/convert_element_type | solution.py:76
  110.6 1.9 constant_dynamic-update-slice_fusion.9
  113.8 5.8 %broadcast_multiply_fusion.3 = (f32[18,10,50,128]{3,2,1,0:T(8,128)S(1)}, f32[18,10,50,128]{3,2,1,0:T(8,128)S(1)}) fusion(f32[18,10,50]{2,1,0:T(8,128)S(1)} %get-tuple-element.157, bf16[18,10,50,512]{3,2,1,0:T(8,128)(2,1)} %get-tuple-element.195, s32[]{:T(128)S(6)} %select_n.5, f32[18,10,50]{2,1,0:T(8,128)S(1)} %get-tuple-element.158), kind=kLoop, calls=%fused_computation.52.clone.1 | loop fusion | flops 3456000 | bytes 11592004 | tf_op jit(solution)/shard_map/while/body/eval_jaxpr/mul | solution.py:59
  120.7 2.1 dynamic-slice_convert_fusion.2
  122.8 2.9 %multiply_add_fusion.3 = (f32[16,10,50,128]{3,2,1,0:T(8,128)S(1)}, f32[16,10,50,128]{3,2,1,0:T(8,128)}) fusion(f32[18,10,50,128]{3,2,1,0:T(8,128)S(1)} %dynamic-slice_convert_fusion.2), kind=kLoop, calls=%fused_computation.8.clone.1 | loop fusion | flops 6144000 | bytes 20480000 | tf_op jit(solution)/shard_map/while/body/eval_jaxpr/add | solution.py:47
  126.3 3.1 %fusion.57 = bf16[16,8,48,128]{3,2,1,0:T(8,128)(2,1)} fusion(f32[16,8,50,128]{3,2,1,0:T(8,128)S(1)} %fusion.55, f32[16,8,50,128]{3,2,1,0:T(8,128)S(1)} %fusion.56, f32[16,8,48]{2,1,0:T(8,128)S(1)} %slice_multiply_fusion.18), kind=kLoop, calls=%fused_computation.28.clone.1 | loop fusion | flops 9437184 | bytes 20471808 | tf_op jit(solution)/shard_map/while/body/eval_jaxpr/convert_element_type | solution.py:76
  130.3 5.2 %fusion.60 = f32[16,8,50,128]{3,2,1,0:T(8,128)S(1)} fusion(f32[16,10,50,128]{3,2,1,0:T(8,128)} %get-tuple-element.162), kind=kLoop, calls=%fused_computation.22.clone.1 | loop fusion | flops 2457600 | bytes 13107200 | tf_op jit(solution)/shard_map/while/body/eval_jaxpr/add | solution.py:47
  135.7 3.6 %fusion.63 = bf16[16,8,48,128]{3,2,1,0:T(8,128)(2,1)S(1)} fusion(f32[18,10,50,128]{3,2,1,0:T(8,128)S(1)} %get-tuple-element.161, f32[16,8,50,128]{3,2,1,0:T(8,128)S(1)} %fusion.59, f32[16,8,50,128]{3,2,1,0:T(8,128)S(1)} %fusion.60, f32[18,10,50,128]{3,2,1,0:T(8,128)S(1)} %dynamic-slice_convert_fusion.2, f32[16,8,48]{2,1,0:T(8,128)S(1)} %get-tuple-element.163, ...), kind=kLoop, calls=%fused_computation.40.clone.1 | loop fusion | flops 14155776 | bytes 26787840 | tf_op jit(solution)/shard_map/while/body/eval_jaxpr/convert_element_type | solution.py:76
  139.3 1.9 constant_dynamic-update-slice_fusion.9
  142.5 5.8 %broadcast_multiply_fusion.3 = (f32[18,10,50,128]{3,2,1,0:T(8,128)S(1)}, f32[18,10,50,128]{3,2,1,0:T(8,128)S(1)}) fusion(f32[18,10,50]{2,1,0:T(8,128)S(1)} %get-tuple-element.157, bf16[18,10,50,512]{3,2,1,0:T(8,128)(2,1)} %get-tuple-element.195, s32[]{:T(128)S(6)} %select_n.5, f32[18,10,50]{2,1,0:T(8,128)S(1)} %get-tuple-element.158), kind=kLoop, calls=%fused_computation.52.clone.1 | loop fusion | flops 3456000 | bytes 11592004 | tf_op jit(solution)/shard_map/while/body/eval_jaxpr/mul | solution.py:59
  149.4 2.1 dynamic-slice_convert_fusion.2
  151.5 2.9 %multiply_add_fusion.3 = (f32[16,10,50,128]{3,2,1,0:T(8,128)S(1)}, f32[16,10,50,128]{3,2,1,0:T(8,128)}) fusion(f32[18,10,50,128]{3,2,1,0:T(8,128)S(1)} %dynamic-slice_convert_fusion.2), kind=kLoop, calls=%fused_computation.8.clone.1 | loop fusion | flops 6144000 | bytes 20480000 | tf_op jit(solution)/shard_map/while/body/eval_jaxpr/add | solution.py:47
  154.9 3.1 %fusion.57 = bf16[16,8,48,128]{3,2,1,0:T(8,128)(2,1)} fusion(f32[16,8,50,128]{3,2,1,0:T(8,128)S(1)} %fusion.55, f32[16,8,50,128]{3,2,1,0:T(8,128)S(1)} %fusion.56, f32[16,8,48]{2,1,0:T(8,128)S(1)} %slice_multiply_fusion.18), kind=kLoop, calls=%fused_computation.28.clone.1 | loop fusion | flops 9437184 | bytes 20471808 | tf_op jit(solution)/shard_map/while/body/eval_jaxpr/convert_element_type | solution.py:76
  158.9 5.2 %fusion.60 = f32[16,8,50,128]{3,2,1,0:T(8,128)S(1)} fusion(f32[16,10,50,128]{3,2,1,0:T(8,128)} %get-tuple-element.162), kind=kLoop, calls=%fused_computation.22.clone.1 | loop fusion | flops 2457600 | bytes 13107200 | tf_op jit(solution)/shard_map/while/body/eval_jaxpr/add | solution.py:47
  164.3 3.6 %fusion.63 = bf16[16,8,48,128]{3,2,1,0:T(8,128)(2,1)S(1)} fusion(f32[18,10,50,128]{3,2,1,0:T(8,128)S(1)} %get-tuple-element.161, f32[16,8,50,128]{3,2,1,0:T(8,128)S(1)} %fusion.59, f32[16,8,50,128]{3,2,1,0:T(8,128)S(1)} %fusion.60, f32[18,10,50,128]{3,2,1,0:T(8,128)S(1)} %dynamic-slice_convert_fusion.2, f32[16,8,48]{2,1,0:T(8,128)S(1)} %get-tuple-element.163, ...), kind=kLoop, calls=%fused_computation.40.clone.1 | loop fusion | flops 14155776 | bytes 26787840 | tf_op jit(solution)/shard_map/while/body/eval_jaxpr/convert_element_type | solution.py:76
  167.9 1.9 constant_dynamic-update-slice_fusion.9
  171.1 5.8 %broadcast_multiply_fusion.3 = (f32[18,10,50,128]{3,2,1,0:T(8,128)S(1)}, f32[18,10,50,128]{3,2,1,0:T(8,128)S(1)}) fusion(f32[18,10,50]{2,1,0:T(8,128)S(1)} %get-tuple-element.157, bf16[18,10,50,512]{3,2,1,0:T(8,128)(2,1)} %get-tuple-element.195, s32[]{:T(128)S(6)} %select_n.5, f32[18,10,50]{2,1,0:T(8,128)S(1)} %get-tuple-element.158), kind=kLoop, calls=%fused_computation.52.clone.1 | loop fusion | flops 3456000 | bytes 11592004 | tf_op jit(solution)/shard_map/while/body/eval_jaxpr/mul | solution.py:59
  178.0 2.1 dynamic-slice_convert_fusion.2
  180.0 2.9 %multiply_add_fusion.3 = (f32[16,10,50,128]{3,2,1,0:T(8,128)S(1)}, f32[16,10,50,128]{3,2,1,0:T(8,128)}) fusion(f32[18,10,50,128]{3,2,1,0:T(8,128)S(1)} %dynamic-slice_convert_fusion.2), kind=kLoop, calls=%fused_computation.8.clone.1 | loop fusion | flops 6144000 | bytes 20480000 | tf_op jit(solution)/shard_map/while/body/eval_jaxpr/add | solution.py:47
  183.5 3.1 %fusion.57 = bf16[16,8,48,128]{3,2,1,0:T(8,128)(2,1)} fusion(f32[16,8,50,128]{3,2,1,0:T(8,128)S(1)} %fusion.55, f32[16,8,50,128]{3,2,1,0:T(8,128)S(1)} %fusion.56, f32[16,8,48]{2,1,0:T(8,128)S(1)} %slice_multiply_fusion.18), kind=kLoop, calls=%fused_computation.28.clone.1 | loop fusion | flops 9437184 | bytes 20471808 | tf_op jit(solution)/shard_map/while/body/eval_jaxpr/convert_element_type | solution.py:76
  187.5 5.2 %fusion.60 = f32[16,8,50,128]{3,2,1,0:T(8,128)S(1)} fusion(f32[16,10,50,128]{3,2,1,0:T(8,128)} %get-tuple-element.162), kind=kLoop, calls=%fused_computation.22.clone.1 | loop fusion | flops 2457600 | bytes 13107200 | tf_op jit(solution)/shard_map/while/body/eval_jaxpr/add | solution.py:47
  192.9 3.6 %fusion.63 = bf16[16,8,48,128]{3,2,1,0:T(8,128)(2,1)S(1)} fusion(f32[18,10,50,128]{3,2,1,0:T(8,128)S(1)} %get-tuple-element.161, f32[16,8,50,128]{3,2,1,0:T(8,128)S(1)} %fusion.59, f32[16,8,50,128]{3,2,1,0:T(8,128)S(1)} %fusion.60, f32[18,10,50,128]{3,2,1,0:T(8,128)S(1)} %dynamic-slice_convert_fusion.2, f32[16,8,48]{2,1,0:T(8,128)S(1)} %get-tuple-element.163, ...), kind=kLoop, calls=%fused_computation.40.clone.1 | loop fusion | flops 14155776 | bytes 26787840 | tf_op jit(solution)/shard_map/while/body/eval_jaxpr/convert_element_type | solution.py:76
  196.5 1.9 constant_dynamic-update-slice_fusion.9
  198.4 7.5 %convolution_bitcast_fusion = f32[512,4,128]{0,2,1:T(8,128)S(1)} fusion(bf16[4,6144,128]{2,1,0:T(8,128)(2,1)} %get-tuple-element.65, bf16[6144,512,1]{1,0,2:T(8,128)(2,1)} %bitcast.39), kind=kOutput, calls=%fused_computation.74 | convolution fusion | flops 3221225472 | bytes 13631488 | tf_op jit(solution)/shard_map/cp,bcq->pbq/dot_general | solution.py:101
  206.3 7.7 %convolution_bitcast_fusion.1 = f32[512,4,128]{0,2,1:T(8,128)S(1)} fusion(bf16[4,6144,128]{2,1,0:T(8,128)(2,1)} %get-tuple-element.64, bf16[6144,512,1]{1,0,2:T(8,128)(2,1)} %bitcast.40), kind=kOutput, calls=%fused_computation.75 | convolution fusion | flops 3221225472 | bytes 13631488 | tf_op jit(solution)/shard_map/cp,bcq->pbq/dot_general | solution.py:98
  214.7 29.5 %all_to_all.15 = f32[4,128,1024]{1,2,0:T(8,128)S(1)} all-to-all(f32[4,128,1024]{1,2,0:T(8,128)S(1)} %pad_maximum_fusion.1), channel_id=1, replica_groups=mesh['gx'=4,'gy'=16,'gz'=2] {'gx'}, dimensions={0} | all-to-all | bytes 4194304 | tf_op jit(solution)/shard_map/all_to_all | solution.py:37
  244.6 20.9 %all_to_all.16 = f32[16,8,1024]{2,1,0:T(8,128)S(1)} all-to-all(f32[16,8,1024]{2,1,0:T(8,128)S(1)} %bitcast.43), channel_id=1, replica_groups=mesh['gx'=4,'gy'=16,'gz'=2] {'gy'}, dimensions={0} | all-to-all | bytes 1048576 | tf_op jit(solution)/shard_map/all_to_all | solution.py:37
  265.5 11.1 %all_to_all.17 = f32[2,4,1024]{2,1,0:T(4,128)S(1)} all-to-all(f32[2,4,1024]{2,1,0:T(4,128)S(1)} %reshape.46), channel_id=1, replica_groups=mesh['gx'=4,'gy'=16,'gz'=2] {'gz'}, dimensions={0} | all-to-all | bytes 65536 | tf_op jit(solution)/shard_map/all_to_all | solution.py:37
  276.6 0.6 slice_multiply_fusion.15
  (87 shorter events, 14.5 us)
Async XLA Ops:
  1.8 9.3 %collective-permute-start.6 = (bf16[1,8,48,512]{3,2,1,0:T(8,128)(2,1)S(1)}, bf16[1,8,48,512]{3,2,1,0:T(8,128)(2,1)S(1)}, u32[]{:S(2)}, u32[]{:S(2)}) collective-permute-start(bf16[1,8,48,512]{3,2,1,0:T(8,128)(2,1)S(1)} %get-tuple-element.95), channel_id=1, source_target_pairs={{0,32},{32,64},{64,96},{1,33},{33,65},{65,97},{2,34},{34,66},{66,9... | collective-permute-start | bytes 1179656 | tf_op jit(solution)/shard_map/ppermute | solution.py:20
  3.8 7.2 %collective-permute-start = (f32[2,1,8,48]{3,2,1,0:T(8,128)S(1)}, f32[2,1,8,48]{3,2,1,0:T(8,128)S(1)}, u32[]{:S(2)}, u32[]{:S(2)}) collective-permute-start(f32[2,1,8,48]{3,2,1,0:T(8,128)S(1)} %get-tuple-element.101), channel_id=1, source_target_pairs={{0,32},{32,64},{64,96},{1,33},{33,65},{65,97},{2,34},{34,66},{66,9... | collective-permute-start | bytes 9224 | tf_op jit(solution)/shard_map/ppermute | solution.py:20
  8.5 17.7 %collective-permute-start.1 = (f32[2,1,8,48]{3,2,1,0:T(8,128)S(1)}, f32[2,1,8,48]{3,2,1,0:T(8,128)S(1)}, u32[]{:S(2)}, u32[]{:S(2)}) collective-permute-start(f32[2,1,8,48]{3,2,1,0:T(8,128)S(1)} %get-tuple-element.100), channel_id=1, source_target_pairs={{32,0},{64,32},{96,64},{33,1},{65,33},{97,65},{34,2},{66,34},{98,6... | collective-permute-start | bytes 9224 | tf_op jit(solution)/shard_map/ppermute | solution.py:22
  9.8 5.2 %collective-permute-start.7 = (bf16[1,8,48,512]{3,2,1,0:T(8,128)(2,1)S(1)}, bf16[1,8,48,512]{3,2,1,0:T(8,128)(2,1)S(1)}, u32[]{:S(2)}, u32[]{:S(2)}) collective-permute-start(bf16[1,8,48,512]{3,2,1,0:T(8,128)(2,1)S(1)} %get-tuple-element.94), channel_id=1, source_target_pairs={{32,0},{64,32},{96,64},{33,1},{65,33},{97,65},{34,2},{66,34},{98,6... | collective-permute-start | bytes 1179656 | tf_op jit(solution)/shard_map/ppermute | solution.py:22
  11.2 15.0 %copy-start.3 = (f32[2,16,8,48]{3,2,1,0:T(8,128)S(1)}, f32[2,16,8,48]{3,2,1,0:T(8,128)}, u32[]{:S(2)}) copy-start(f32[2,16,8,48]{3,2,1,0:T(8,128)} %param.5) | copy-start | bytes 147460
  15.1 2.9 %copy-start.1 = (bf16[18,8,48,512]{3,2,1,0:T(8,128)(2,1)}, bf16[18,8,48,512]{3,2,1,0:T(8,128)(2,1)S(1)}, u32[]{:S(2)}) copy-start(bf16[18,8,48,512]{3,2,1,0:T(8,128)(2,1)S(1)} %constant_dynamic-update-slice_fusion.5) | copy-start | bytes 21233668
  19.4 37.6 %collective-permute-start.9 = (bf16[18,1,48,512]{3,2,1,0:T(8,128)(2,1)}, bf16[18,1,48,512]{3,2,1,0:T(8,128)(2,1)}, u32[]{:S(2)}, u32[]{:S(2)}) collective-permute-start(bf16[18,1,48,512]{3,2,1,0:T(8,128)(2,1)} %get-tuple-element.93), channel_id=1, source_target_pairs={{2,0},{4,2},{6,4},{8,6},{10,8},{12,10},{14,12},{16,14},{18,16},{20... | collective-permute-start | bytes 2654216 | tf_op jit(solution)/shard_map/ppermute | solution.py:22
  20.7 36.3 %collective-permute-start.8 = (bf16[18,1,48,512]{3,2,1,0:T(8,128)(2,1)}, bf16[18,1,48,512]{3,2,1,0:T(8,128)(2,1)}, u32[]{:S(2)}, u32[]{:S(2)}) collective-permute-start(bf16[18,1,48,512]{3,2,1,0:T(8,128)(2,1)} %get-tuple-element.92), channel_id=1, source_target_pairs={{0,2},{2,4},{4,6},{6,8},{8,10},{10,12},{12,14},{14,16},{16,18},{18... | collective-permute-start | bytes 2654216 | tf_op jit(solution)/shard_map/ppermute | solution.py:20
  26.1 48.3 %slice-start = ((s8[7077888]{0:T(1024)(128)(4,1)}), s8[2883584]{0:T(1024)(128)(4,1)S(1)}, s32[]{:S(2)}) async-start(s8[7077888]{0:T(1024)(128)(4,1)} %bitcast.41), calls=%async_computation.3 | async-start | bytes 5767168
  26.2 14.2 %collective-permute-start.3 = (f32[2,18,1,48]{3,2,1,0:T(1,128)S(1)}, f32[2,18,1,48]{3,2,1,0:T(1,128)S(1)}, u32[]{:S(2)}, u32[]{:S(2)}) collective-permute-start(f32[2,18,1,48]{3,2,1,0:T(1,128)S(1)} %get-tuple-element.99), channel_id=1, source_target_pairs={{2,0},{4,2},{6,4},{8,6},{10,8},{12,10},{14,12},{16,14},{18,16},{20... | collective-permute-start | bytes 20744 | tf_op jit(solution)/shard_map/ppermute | solution.py:22
  27.8 14.4 %collective-permute-start.2 = (f32[2,18,1,48]{3,2,1,0:T(1,128)S(1)}, f32[2,18,1,48]{3,2,1,0:T(1,128)S(1)}, u32[]{:S(2)}, u32[]{:S(2)}) collective-permute-start(f32[2,18,1,48]{3,2,1,0:T(1,128)S(1)} %get-tuple-element.98), channel_id=1, source_target_pairs={{0,2},{2,4},{4,6},{6,8},{8,10},{10,12},{12,14},{14,16},{16,18},{18... | collective-permute-start | bytes 20744 | tf_op jit(solution)/shard_map/ppermute | solution.py:20
  43.2 10.6 %collective-permute-start.5 = (f32[2,18,10,1]{3,2,1,0:T(8,128)}, f32[2,18,10,1]{3,2,1,0:T(8,128)S(1)}, u32[]{:S(2)}, u32[]{:S(2)}) collective-permute-start(f32[2,18,10,1]{3,2,1,0:T(8,128)} %get-tuple-element.97), channel_id=1, source_target_pairs={{1,0},{3,2},{5,4},{7,6},{9,8},{11,10},{13,12},{15,14},{17,16},{19,... | collective-permute-start | bytes 4328 | tf_op jit(solution)/shard_map/ppermute | solution.py:22
  44.5 11.2 %collective-permute-start.4 = (f32[2,18,10,1]{3,2,1,0:T(8,128)}, f32[2,18,10,1]{3,2,1,0:T(8,128)}, u32[]{:S(2)}, u32[]{:S(2)}) collective-permute-start(f32[2,18,10,1]{3,2,1,0:T(8,128)} %get-tuple-element.96), channel_id=1, source_target_pairs={{0,1},{2,3},{4,5},{6,7},{8,9},{10,11},{12,13},{14,15},{16,17},{18,... | collective-permute-start | bytes 4328 | tf_op jit(solution)/shard_map/ppermute | solution.py:20
  53.8 0.7 copy-start.2
  57.0 17.5 %slice-start.1 = ((s8[7077888]{0:T(1024)(128)(4,1)}), s8[4194304]{0:T(1024)(128)(4,1)S(1)}, s32[]{:S(2)}) async-start(s8[7077888]{0:T(1024)(128)(4,1)} %bitcast.41), calls=%async_computation.4 | async-start | bytes 8388608
  59.6 13.1 %collective-permute-start.11 = (bf16[18,10,1,512]{3,2,1,0:T(2,128)(2,1)S(1)}, bf16[18,10,1,512]{3,2,1,0:T(2,128)(2,1)S(1)}, u32[]{:S(2)}, u32[]{:S(2)}) collective-permute-start(bf16[18,10,1,512]{3,2,1,0:T(2,128)(2,1)S(1)} %get-tuple-element.91), channel_id=1, source_target_pairs={{1,0},{3,2},{5,4},{7,6},{9,8},{11,10},{13,12},{15,14},{17,16},{19,... | collective-permute-start | bytes 552968 | tf_op jit(solution)/shard_map/ppermute | solution.py:22
  60.9 13.6 %collective-permute-start.10 = (bf16[18,10,1,512]{3,2,1,0:T(2,128)(2,1)S(1)}, bf16[18,10,1,512]{3,2,1,0:T(2,128)(2,1)S(1)}, u32[]{:S(2)}, u32[]{:S(2)}) collective-permute-start(bf16[18,10,1,512]{3,2,1,0:T(2,128)(2,1)S(1)} %get-tuple-element.90), channel_id=1, source_target_pairs={{0,1},{2,3},{4,5},{6,7},{8,9},{10,11},{12,13},{14,15},{16,17},{18,... | collective-permute-start | bytes 552968 | tf_op jit(solution)/shard_map/ppermute | solution.py:20
  107.0 3.6 %copy-start = (bf16[16,8,48,128]{3,2,1,0:T(8,128)(2,1)S(1)}, bf16[16,8,48,128]{3,2,1,0:T(8,128)(2,1)}, u32[]{:S(2)}) copy-start(bf16[16,8,48,128]{3,2,1,0:T(8,128)(2,1)} %fusion.57) | copy-start | bytes 4718596 | tf_op jit(solution)/shard_map/while
  135.7 3.6 %copy-start = (bf16[16,8,48,128]{3,2,1,0:T(8,128)(2,1)S(1)}, bf16[16,8,48,128]{3,2,1,0:T(8,128)(2,1)}, u32[]{:S(2)}) copy-start(bf16[16,8,48,128]{3,2,1,0:T(8,128)(2,1)} %fusion.57) | copy-start | bytes 4718596 | tf_op jit(solution)/shard_map/while
  164.3 3.6 %copy-start = (bf16[16,8,48,128]{3,2,1,0:T(8,128)(2,1)S(1)}, bf16[16,8,48,128]{3,2,1,0:T(8,128)(2,1)}, u32[]{:S(2)}) copy-start(bf16[16,8,48,128]{3,2,1,0:T(8,128)(2,1)} %fusion.57) | copy-start | bytes 4718596 | tf_op jit(solution)/shard_map/while
  192.9 3.6 %copy-start = (bf16[16,8,48,128]{3,2,1,0:T(8,128)(2,1)S(1)}, bf16[16,8,48,128]{3,2,1,0:T(8,128)(2,1)}, u32[]{:S(2)}) copy-start(bf16[16,8,48,128]{3,2,1,0:T(8,128)(2,1)} %fusion.57) | copy-start | bytes 4718596 | tf_op jit(solution)/shard_map/while
where the time goes:
time: 279 us; the launch traced here: 277 us
  other arithmetic  116 us (42%)
  blocking collectives  61.6 us (22%)
  starting transfers between devices  37 us (13%)
  local copies, waits for them, and re-layouts  23 us (8%)
  waiting for transfers between devices  20.8 us (7%)
  matrix products  15.2 us (5%)
  loops' own time  3.05 us (1%)
    all_to_all x3, blocking collectives, sum_at_owner(): parts = lax.all_to_all(split_up(x, dim, devices), axis, 0, 0, tiled=True)  61.6 us
    add x37, other arithmetic, three_taps(): field = side * (lower + upper) + middle * centre  42.4 us
    ppermute x6, starting transfers between devices, with_halo(): lax.ppermute(tail, axis, [(i, (i + 1) % count) for i in range(ends)])  29 us
    convert_element_type x8, other arithmetic, apply_operators(): return (stiff_sum.astype(jnp.bfloat16), mass_sum.astype(jnp.bfloat16))  26.6 us
    mul x4, other arithmetic, apply_operators(): rho_values = rho[..., None] * values  23.2 us
    ppermute x6, waiting for transfers between devices, with_halo(): lax.ppermute(head, axis, [((i + 1) % count, i) for i in range(ends)])  16.2 us
    concatenate x3, other arithmetic, with_halo(): jnp.concatenate([lax.ppermute(tail, axis, [(i, (i + 1) % count) for i in...  10.9 us
    convert_element_type x4, other arithmetic, apply_operators(): values = padded.astype(jnp.float32)  8.28 us
  transfers between devices with their start and end apart: 12, of which 6 were waited for; matrix products, arithmetic and copies ran while one was open for 3% of the time, Pallas kernels for 0%

commit v1 on v0

v1 whole, which is shorter than its diff:
```python
import jax
import jax.numpy as jnp
import numpy as np
from jax import lax
from jax.experimental import pallas as pl
from jax.experimental.pallas import tpu as pltpu
from jax.sharding import PartitionSpec as P

MESH = pl.DeviceIdType.MESH
F32, BF16 = jnp.float32, jnp.bfloat16
PC, PM = 1.0 / 16.0, 1.0 / 216.0


def taps(rows, cols, middle):
    gap = np.abs(rows[:, None] - cols[None, :])
    return np.where(gap == 0, middle, np.where(gap == 1, 1, 0))


def pair_weights(halo, own, middle):
    total = 1
    for h, o in zip(halo, own):
        total = total * taps(h, o, middle)
    return total


def grid(*axes):
    return [a.reshape(-1) for a in np.meshgrid(*axes, indexing="ij")]


def stacked(halo, own, pad):
    w = np.concatenate([pair_weights(halo, own, 2), pair_weights(halo, own, 4)], axis=1)
    w = np.concatenate([w, np.zeros((pad, w.shape[1]), w.dtype)], axis=0)
    return w.astype(np.float32)


def weight_arrays(nx, ny, nz):
    hx = nx // 2
    y, z = grid(np.arange(ny), np.arange(nz))
    plane = stacked([y, z], [y, z], 0)
    hxx, hzz = grid(np.arange(-1, hx + 1), np.arange(nz))
    oxx, ozz = grid(np.arange(hx), np.arange(nz))
    wy = stacked(
        [hxx, hzz, 0 * hxx + 1], [oxx, ozz, 0 * oxx], (-hxx.size) % 128
    )
    wx = stacked([y, z, 0 * y + 1], [y, z, 0 * y], 0)
    far = 99
    slabs = []
    xs = np.arange(nx)
    for yy in range(ny):
        slabs.append((xs, 0 * xs + yy))
    ys = np.concatenate([np.arange(ny), far + 0 * np.arange(nx - ny)])
    first = np.where(xs == 0, 0, far)
    last = np.where(xs == nx - 1, 0, far)
    slabs += [(xs, 0 * xs - 1), (xs, 0 * xs + ny)]
    slabs += [(0 * xs - 1, ys), (0 * xs + nx, ys)]
    slabs += [(last - 1, 0 * xs - 1), (last - 1, 0 * xs + ny)]
    slabs += [(first + nx, 0 * xs - 1), (first + nx, 0 * xs + ny)]
    zx = np.concatenate([s[0] for s in slabs])
    zy = np.concatenate([s[1] for s in slabs])
    oyy, oxx = grid(np.arange(ny), np.arange(nx))
    wz = stacked([zx, zy, 0 * zx + 1], [oxx, oyy, 0 * oxx], 0)
    return plane, wy, wx, wz


def nt(a, b):
    return lax.dot_general(a, b, (((1,), (1,)), ((), ())), preferred_element_type=F32)


def nn(a, b):
    return jnp.dot(a, b, preferred_element_type=F32)


def exact(a, b):
    return jnp.dot(a, b, preferred_element_type=F32, precision=lax.Precision.HIGHEST)


def exact_nt(a, b):
    return lax.dot_general(
        a, b, (((1,), (1,)), ((), ())), preferred_element_type=F32,
        precision=lax.Precision.HIGHEST,
    )


def local_kernel(
    dims, scale,
    v_ref, mat_ref, faces_ref, zf_ref, zx_ref, wp_ref, wy_ref, wx_ref, wz_ref,
    out_ref,
    vbuf, vt, fbuf, ym, acc, hy, hx, hz, fh, vsem, send_sem, recv_sem,
):
    nx, ny, nz, cols, ngx, ngy = dims
    n = ny * nz
    gx, gy, gz = lax.axis_index("gx"), lax.axis_index("gy"), lax.axis_index("gz")
    hx_n = nx // 2

    loads = [pltpu.make_async_copy(v_ref.at[x], vbuf.at[x], vsem.at[x]) for x in range(nx)]
    for load in loads:
        load.start()

    def zrow(k):
        return hz.at[k]

    links = [
        ((0, 1), False, v_ref.at[:, ny - 1], hy.at[pl.ds(1, nx)]),
        ((1, 1), False, v_ref.at[nx - 1, ny - 1], hy.at[0]),
        ((-1, 1), False, v_ref.at[0, ny - 1], hy.at[nx + 1]),
        ((1, 0), False, v_ref.at[nx - 1], hx),
        ((0, 0), True, zf_ref, hz.at[pl.ds(0, ny)]),
        ((0, 1), True, zf_ref.at[ny - 1], zrow(ny)),
        ((0, -1), True, zf_ref.at[0], zrow(ny + 1)),
        ((1, 0), True, zx_ref.at[1], zrow(ny + 2)),
        ((-1, 0), True, zx_ref.at[0], zrow(ny + 3)),
        ((1, 1), True, zf_ref.at[ny - 1], zrow(ny + 4)),
        ((1, -1), True, zf_ref.at[0], zrow(ny + 5)),
        ((-1, 1), True, zf_ref.at[ny - 1], zrow(ny + 6)),
        ((-1, -1), True, zf_ref.at[0], zrow(ny + 7)),
    ]

    def inside(dx, dy):
        ok = None
        for move, at, count in ((dx, gx, ngx), (dy, gy, ngy)):
            here = None
            if move == 1:
                here = at < count - 1
            if move == -1:
                here = at > 0
            if here is not None:
                ok = here if ok is None else jnp.logical_and(ok, here)
        return ok

    def both(a, b):
        return b if a is None else jnp.logical_and(a, b)

    def sends_if(link):
        (dx, dy), cut, _, _ = link
        ok = inside(dx, dy)
        return both(ok, gz == 0) if cut else ok

    def gets_if(link):
        (dx, dy), cut, _, _ = link
        ok = inside(-dx, -dy)
        return both(ok, gz == 1) if cut else ok

    hy[...] = jnp.zeros_like(hy)
    hx[...] = jnp.zeros_like(hx)
    hz[...] = jnp.zeros_like(hz)
    fh[...] = jnp.zeros_like(fh)

    barrier = pltpu.get_barrier_semaphore()
    targets = 0
    for link in links:
        (dx, dy), cut, _, _ = link
        source = (gx - dx, gy - dy, 0 if cut else gz)

        @pl.when(gets_if(link))
        def _(source=source):
            pl.semaphore_signal(barrier, inc=1, device_id=source, device_id_type=MESH)

        targets = targets + sends_if(link).astype(jnp.int32)

    @pl.when(targets > 0)
    def _():
        pl.semaphore_wait(barrier, targets)

    copies = []
    for k, link in enumerate(links):
        (dx, dy), cut, source, target = link
        device = (gx + dx, gy + dy, 1 if cut else gz)
        pair = [
            pltpu.make_async_remote_copy(
                src_ref=s, dst_ref=t, send_sem=send_sem.at[2 * k + j],
                recv_sem=recv_sem.at[2 * k + j], device_id=device, device_id_type=MESH,
            )
            for j, (s, t) in enumerate(((faces_ref, fh.at[k]), (source, target)))
        ]
        copies.append(pair)

        @pl.when(sends_if(link))
        def _(pair=pair):
            for copy in pair:
                copy.start()

    kappa, rho = mat_ref[0], mat_ref[1]
    filtered = exact(kappa, wp_ref[:, :n].astype(F32))
    zero = jnp.zeros((1, n), F32)
    around = (
        jnp.concatenate([zero, filtered[:-1]], axis=0)
        + 2.0 * filtered
        + jnp.concatenate([filtered[1:], zero], axis=0)
    )
    diag = 0.5 * (3.5 * kappa + PC * around - 0.5 * kappa)
    coef_v = diag + 0.5 * kappa
    coef_s = PC * kappa
    coef_m = PM * rho

    def stage_a(x):
        if x >= nx:
            return
        loads[x].wait()
        t = vbuf[x].reshape(n, cols).T
        vt[x // 2, :, (x % 2) * n : (x % 2 + 1) * n] = t
        fbuf[x % 6] = nn(t, wp_ref[...])

    chunk = 64

    def stage_b(x):
        half = (x % 2) * n
        buf = (x // 2) % 2
        cv, cs, cm = (c[x : x + 1, :] for c in (coef_v, coef_s, coef_m))
        for r in range(0, cols, chunk):
            rows = slice(r, r + chunk)
            mid_s = fbuf[x % 6, rows, :n]
            mid_m = fbuf[x % 6, rows, n:]
            s, m = 2.0 * mid_s, 4.0 * mid_m
            for near in (x - 1, x + 1):
                if 0 <= near < nx:
                    s = s + fbuf[near % 6, rows, :n]
                    m = m + fbuf[near % 6, rows, n:]
            v = vt[x // 2, rows, half : half + n].astype(F32)
            ym[buf, rows, half : half + n] = (cv * v - cs * s).astype(BF16)
            ym[buf, cols + r : cols + r + chunk, half : half + n] = (cm * m).astype(BF16)

    def stage_c(pair):
        for h in range(2):
            part = nt(vt[pair], ym[pair % 2, h * cols : (h + 1) * cols])
            if pair == 0:
                acc[h] = part
            else:
                acc[h] += part

    pairs = nx // 2
    for x in range(3):
        stage_a(x)
    for i in range(pairs):
        stage_a(2 * i + 3)
        stage_a(2 * i + 4)
        stage_b(2 * i)
        stage_b(2 * i + 1)
        if i > 0:
            stage_c(i - 1)
    stage_c(pairs - 1)

    for k, link in enumerate(links):
        @pl.when(gets_if(link))
        def _(k=k):
            for copy in copies[k]:
                copy.wait_recv()

    def group(halo, kh, rh, own, ko, ro, w_ref):
        m = own.shape[1]
        wc, wm = w_ref[:, :m], w_ref[:, m:]
        ht = halo.T
        plain = nn(ht, w_ref[...])
        h32 = ht.astype(F32)
        by_kappa = nn((h32 * kh).astype(BF16), wc)
        by_rho = nn((h32 * rh).astype(BF16), wm)
        wc32 = wc.astype(F32)
        own_diag = (0.5 * PC) * exact(jnp.broadcast_to(kh, (8, kh.shape[1])), wc32)[:1]
        far_diag = (0.5 * PC) * exact_nt(jnp.broadcast_to(ko, (8, m)), wc32)[:1]
        us = own_diag * own.astype(F32) - PC * (ko * plain[:, :m] + by_kappa)
        um = PM * (ro * plain[:, m:] + by_rho)
        acc[0] += nt(own, us.astype(BF16)) + nt(ht, (far_diag * h32).astype(BF16))
        acc[1] += nt(own, um.astype(BF16))

    def row(k, r, lo, hi):
        return fh[k, r : r + 1, lo:hi]

    def wide(x):
        return jnp.concatenate(x, axis=1)

    kp = wy_ref.shape[0]
    used = (hx_n + 2) * nz
    blank = jnp.zeros((1, kp - used), F32)
    edge = (nx - 1) * nz
    for side in range(2):
        if side == 0:
            pick = lambda r: wide([row(1, r, edge, edge + nz), row(0, r, 0, used - nz), blank])
        else:
            pick = lambda r: wide(
                [row(0, r, (hx_n - 1) * nz, nx * nz), row(2, r, 0, nz), blank]
            )
        slots = -(-kp // nz)
        start = side * hx_n
        halo = hy[start : start + slots].reshape(slots * nz, cols)[:kp]
        own = vbuf[start : start + hx_n, 0].reshape(hx_n * nz, cols).T
        mine = [
            wide([mat_ref[j, x : x + 1, :nz] for x in range(start, start + hx_n)])
            for j in range(2)
        ]
        group(halo, pick(0), pick(1), own, mine[0], mine[1], wy_ref)

    group(
        hx[...].reshape(n, cols), row(3, 2, 0, n), row(3, 3, 0, n),
        vt[0, :, :n], kappa[:1], rho[:1], wx_ref,
    )

    nf = nx * ny
    low, high = (nf - nx, nf), (0, nx)

    def zpick(r):
        spans = [(4, (0, nf)), (5, low), (6, high), (7, (nf + nx, nf + 2 * nx)),
                 (8, (nf, nf + nx)), (9, low), (10, high), (11, low), (12, high)]
        return wide([row(k, r, lo, hi) for k, (lo, hi) in spans])

    group(
        hz[...].reshape((ny + 8) * nx, cols), zpick(4), zpick(5),
        zf_ref[...].reshape(nf, cols).T, faces_ref[4:5, :nf], faces_ref[5:6, :nf], wz_ref,
    )

    for h in range(2):
        total = acc[h]
        out_ref[:, h * cols : (h + 1) * cols] = (total + total.T) * scale

    for k, link in enumerate(links):
        @pl.when(sends_if(link))
        def _(k=k):
            for copy in copies[k]:
                copy.wait_send()


def local_sums(eigvecs, material):
    nx, ny, nz, cols = eigvecs.shape
    n = ny * nz
    count = {a: lax.axis_size(a) for a in ("gx", "gy", "gz")}
    cells = nx * ny * nz * count["gx"] * count["gy"] * count["gz"]
    plane, wy, wx, wz = (jnp.asarray(w, BF16) for w in weight_arrays(nx, ny, nz))
    at = jnp.where(lax.axis_index("gz") == 0, nz - 1, 0)
    zface = lax.dynamic_index_in_dim(eigvecs, at, 2, False)
    zf = jnp.swapaxes(zface, 0, 1)
    zx = jnp.pad(zface[:: nx - 1], ((0, 0), (0, nx - ny), (0, 0)))
    mz = lax.dynamic_index_in_dim(material, at, 3, False)
    flat = material.reshape(2, nx, n)
    width = nx * nz

    def fit(a):
        a = a.reshape(2, -1)
        return jnp.pad(a, ((0, 0), (0, width - a.shape[1])))

    mzx = jnp.pad(mz[:, :: nx - 1], ((0, 0), (0, 0), (0, nx - ny)))
    faces = jnp.concatenate(
        [
            fit(material[:, :, ny - 1]),
            fit(material[:, nx - 1]),
            fit(jnp.concatenate([jnp.swapaxes(mz, 1, 2).reshape(2, -1), mzx.reshape(2, -1)], 1)),
            jnp.zeros((2, width), F32),
        ],
        axis=0,
    )
    anyspace = pl.BlockSpec(memory_space=pl.ANY)
    vmem = pl.BlockSpec(memory_space=pltpu.VMEM)
    kernel = lambda *refs: local_kernel(
        (nx, ny, nz, cols, count["gx"], count["gy"]), 0.5 / cells, *refs
    )
    return pl.pallas_call(
        kernel,
        out_shape=jax.ShapeDtypeStruct((cols, 2 * cols), F32),
        in_specs=[anyspace] + [vmem] * 8,
        out_specs=vmem,
        scratch_shapes=[
            pltpu.VMEM((nx, ny, nz, cols), BF16),
            pltpu.VMEM((nx // 2, cols, 2 * n), BF16),
            pltpu.VMEM((6, cols, 2 * n), F32),
            pltpu.VMEM((2, 2 * cols, 2 * n), BF16),
            pltpu.VMEM((2, cols, cols), F32),
            pltpu.VMEM((nx + 3, nz, cols), BF16),
            pltpu.VMEM((ny, nz, cols), BF16),
            pltpu.VMEM((ny + 8, nx, cols), BF16),
            pltpu.VMEM((13, 8, width), F32),
            pltpu.SemaphoreType.DMA((nx,)),
            pltpu.SemaphoreType.DMA((26,)),
            pltpu.SemaphoreType.DMA((26,)),
        ],
        compiler_params=pltpu.CompilerParams(
            collective_id=0, has_side_effects=True, vmem_limit_bytes=63 * 1024 * 1024
        ),
        name="local_sums",
    )(eigvecs, flat, faces, zf, zx, plane, wy, wx, wz)


def split_up(x, dim, devices):
    dims = x.shape
    parts = x.reshape(*dims[:dim], devices, dims[dim] // devices, *dims[dim + 1 :])
    return jnp.moveaxis(parts, dim, 0)


def sum_at_owner(x, axis, dim):
    devices = lax.axis_size(axis)
    parts = lax.all_to_all(split_up(x, dim, devices), axis, 0, 0, tiled=True)
    return jnp.sum(parts, axis=0)


def per_device(eigvecs, material):
    columns = eigvecs.shape[3]
    part = local_sums(eigvecs, material)
    summed = sum_at_owner(sum_at_owner(sum_at_owner(part, "gx", 0), "gy", 0), "gz", 0)
    return summed[:, :columns], summed[:, columns:]


def solution(mesh):
    return jax.shard_map(
        per_device,
        mesh=mesh,
        in_specs=(P("gx", "gy", "gz", None), P(None, "gx", "gy", "gz")),
        out_specs=(P(("gx", "gy", "gz"), None), P(("gx", "gy", "gz"), None)),
        check_vma=False,
    )
```

time: 279 us -> 110 us (0.39)
  other arithmetic: 116 us -> 0.91 us
  Pallas kernels: 0 us -> 42.3 us
  starting transfers between devices: 37 us -> 0 us
  waiting for transfers between devices: 20.8 us -> 0 us
  matrix products: 15.2 us -> 0 us
  local copies, waits for them, and re-layouts: 23 us -> 8.63 us
  blocking collectives: 61.6 us -> 57.1 us
  loops' own time: 3.05 us -> 0 us
    add x37 -> x0, other arithmetic: 42.4 us -> none  [three_taps(): field = side * (lower + upper) + middle * centre]
    pallas_call x0 -> x1, Pallas kernels: none -> 42.3 us  [local_sums(): pl.pallas_call(kernel, out_shape=jax.ShapeDtypeStruct((cols, 2 * cols), F...]
    ppermute x12 -> x0, starting transfers between devices: 37 us -> none  [the longest x6 29 us: with_halo(): lax.ppermute(tail, axis, [(i, (i + 1) % count) for i in range(ends)])]
    convert_element_type x12 -> x0, other arithmetic: 34.9 us -> none  [the longest x8 26.6 us: apply_operators(): return (stiff_sum.astype(jnp.bfloat16), mass_sum.astype(jnp.bfloat16))]
    mul x12 -> x0, other arithmetic: 24 us -> none  [the longest x4 23.2 us: apply_operators(): rho_values = rho[..., None] * values]
    ppermute x12 -> x0, waiting for transfers between devices: 20.8 us -> none  [the longest x6 16.2 us: with_halo(): lax.ppermute(head, axis, [((i + 1) % count, i) for i in range(ends)])]
    dot_general x2 -> x0, matrix products: 15.2 us -> none  [the longest x1 7.74 us: per_device(): jnp.einsum('cp,bcq->pbq', flat_vectors, stiff_blocks, preferred_element_t...]
    concatenate x4 -> x2, other arithmetic: 11 us -> 0.68 us  [the longest x1 0.67 us: local_sums(): jnp.concatenate([fit(material[:, :, ny - 1]), fit(material[:, nx - 1]), f...]
  transfers between devices with their start and end apart: 12 -> 0, of which waited for: 6 -> 0; matrix products, arithmetic and copies ran while one was open for 3% -> 0% of each run, Pallas kernels for 0% -> 0%
where the time goes in v1:
time: 110 us
  blocking collectives  57.1 us (52%)
  Pallas kernels  42.3 us (38%)
  local copies, waits for them, and re-layouts  8.63 us (8%)
    all_to_all x3, blocking collectives, sum_at_owner(): parts = lax.all_to_all(split_up(x, dim, devices), axis, 0, 0, tiled=True)  57.1 us
    pallas_call x1, Pallas kernels, local_sums(): pl.pallas_call(kernel, out_shape=jax.ShapeDtypeStruct((cols, 2 * cols), F...  42.3 us

profile of v1, /device:TPU:0, one launch (start us, length us, event | category | flops | bytes accessed | tf_op | source)
XLA Modules:
  0.0 109.6 jit_solution(14052436922727393410)
XLA Ops:
  0.6 0.7 slice.19
  1.3 1.0 slice_reduce_fusion
  2.3 1.6 %reshape.22.refs_1_ = f32[2,16,384]{2,1,0:T(8,128)} reshape(f32[2,16,8,48]{3,2,1,0:T(8,128)} %param.7) | data formatting | bytes 98304 | tf_op jit(solution)/shard_map/reshape | solution.py:331
  3.9 1.0 constant_dynamic-slice_fusion.1
  4.9 1.5 %constant_dynamic-slice_fusion = bf16[16,8,1,512]{3,2,1,0:T(2,128)(2,1)S(1)} fusion(bf16[16,8,48,512]{3,2,1,0:T(8,128)(2,1)} %refs_0_.1, s32[]{:T(128)S(6)} %select_n.8), kind=kLoop, calls=%fused_computation.10 | loop fusion | bytes 262148 | tf_op jit(solution)/shard_map/jit(dynamic_index_in_dim)/dynamic_slice | solution.py:327
  6.5 0.8 copy.24
  7.3 0.1 reshape_squeeze.7
  7.4 0.1 reshape_squeeze.6
  7.5 0.2 copy.18
  7.6 0.1 reshape.23
  7.7 0.1 slice.20
  7.8 0.1 copy.20
  7.9 0.1 reshape.24
  8.0 0.1 pad.23.clone
  8.1 0.6 pad.19.refs_4_
  8.7 0.7 fusion.1.refs_2_
  9.4 42.3 %local_sums.1 = f32[512,1024]{1,0:T(8,128)} custom-call(bf16[16,8,48,512]{3,2,1,0:T(8,128)(2,1)} %refs_0_.1, f32[2,16,384]{2,1,0:T(8,128)} %reshape.22.refs_1_, f32[8,768]{1,0:T(8,128)} %fusion.1.refs_2_, bf16[8,16,512]{2,1,0:T(8,128)(2,1)} %bitcast.19, bf16[2,16,512]{2,1,0:T(8,128)(2,1)} %pad.19.refs_4_, bf16[384,768]{1,0:T(8,128)(2,1)} %constant.29.clone.refs_5_.refs_7_, ...), custom_call_target="tpu_custom_call" | custom-call | tf_op jit(solution)/shard_map/local_sums/pallas_call | solution.py:353
  51.7 29.3 %all_to_all.15 = f32[4,128,1024]{2,1,0:T(8,128)S(1)} all-to-all(f32[4,128,1024]{2,1,0:T(8,128)} %bitcast.17), channel_id=1, replica_groups=mesh['gx'=4,'gy'=16,'gz'=2] {'gx'}, dimensions={0} | all-to-all | bytes 4194304 | tf_op jit(solution)/shard_map/all_to_all | solution.py:387
  80.9 0.2 reduce_sum.27
  81.1 17.7 %all_to_all.16 = f32[16,8,1024]{2,1,0:T(8,128)S(1)} all-to-all(f32[16,8,1024]{2,1,0:T(8,128)S(1)} %bitcast.18), channel_id=1, replica_groups=mesh['gx'=4,'gy'=16,'gz'=2] {'gy'}, dimensions={0} | all-to-all | bytes 1048576 | tf_op jit(solution)/shard_map/all_to_all | solution.py:387
  98.9 10.1 %all_to_all.17 = f32[2,4,1024]{2,1,0:T(4,128)S(1)} all-to-all(f32[2,4,1024]{2,1,0:T(4,128)S(1)} %reshape.27), channel_id=1, replica_groups=mesh['gx'=4,'gy'=16,'gz'=2] {'gz'}, dimensions={0} | all-to-all | bytes 65536 | tf_op jit(solution)/shard_map/all_to_all | solution.py:387
  109.0 0.6 fusion.3
  (8 shorter events, 0.1 us)

commit v2 on v1

--- a/solution.py
+++ b/solution.py
@@ -81,12 +81,62 @@
     )
 
 
+ORDERS = ("yxz", "xzy", "zyx", "xyz")
+GONE = {"x": "x", "y": "y", "z": "lh"}
+SIZE = {"l": 2, "h": 2, "x": 4, "y": 4}
+tiles = len(ORDERS)
+
+
+def exchange_start(t, s, held, pick, place, device_of, send, stage):
+    buf, dims = held
+    dim = ORDERS[t][s]
+    copies = []
+    for j in range(3):
+        at = lax.rem(place[dim] + j + 1, 4)
+        copies.append(
+            send(
+                buf.at[pick(buf, dims, dim, at)], stage[s + 1][t].at[j],
+                tiles + (s * tiles + t) * 3 + j, device_of(dim, at),
+            )
+        )
+    return copies
+
+
+def partners(gx, gy, gz):
+    core, z = lax.rem(gx, 2), gz * 2 + gx // 2
+    x, y = gy // 4, lax.rem(gy, 4)
+    found = [(gx + 1 - 2 * core, gy, gz)]
+    for j in range(1, 4):
+        found.append((gx, x * 4 + lax.rem(y + j, 4), gz))
+        found.append((gx, lax.rem(x + j, 4) * 4 + y, gz))
+        zz = lax.rem(z + j, 4)
+        found.append((lax.rem(zz, 2) * 2 + core, gy, zz // 2))
+    return found
+
+
+def stage_shapes():
+    shapes, keeps = [[(2, 4, 4, 2, 8, 128)] * tiles], []
+    for s in range(3):
+        row, kept = [], []
+        for t in range(tiles):
+            gone = "".join(GONE[d] for d in ORDERS[t][: s + 1])
+            left = tuple(SIZE[d] for d in "lxyh" if d not in gone) + (8, 128)
+            row.append((3,) + left)
+            kept.append(left)
+        shapes.append(row)
+        keeps.append(kept)
+    return shapes, keeps[:2]
+
+
 def local_kernel(
     dims, scale,
     v_ref, mat_ref, faces_ref, zf_ref, zx_ref, wp_ref, wy_ref, wx_ref, wz_ref,
-    out_ref,
+    stiff_ref, mass_ref,
     vbuf, vt, fbuf, ym, acc, hy, hx, hz, fh, vsem, send_sem, recv_sem,
+    q, rsend, rrecv, *rest,
 ):
+    stage = [rest[s * tiles : (s + 1) * tiles] for s in range(4)]
+    keep = [rest[(4 + s) * tiles : (5 + s) * tiles] for s in range(2)]
     nx, ny, nz, cols, ngx, ngy = dims
     n = ny * nz
     gx, gy, gz = lax.axis_index("gx"), lax.axis_index("gy"), lax.axis_index("gz")
@@ -156,10 +206,9 @@
             pl.semaphore_signal(barrier, inc=1, device_id=source, device_id_type=MESH)
 
         targets = targets + sends_if(link).astype(jnp.int32)
-
-    @pl.when(targets > 0)
-    def _():
-        pl.semaphore_wait(barrier, targets)
+    for device in partners(gx, gy, gz):
+        pl.semaphore_signal(barrier, inc=1, device_id=device, device_id_type=MESH)
+    pl.semaphore_wait(barrier, targets + 10)
 
     copies = []
     for k, link in enumerate(links):
@@ -306,10 +355,78 @@
         zf_ref[...].reshape(nf, cols).T, faces_ref[4:5, :nf], faces_ref[5:6, :nf], wz_ref,
     )
 
+    sums = []
     for h in range(2):
         total = acc[h]
-        out_ref[:, h * cols : (h + 1) * cols] = (total + total.T) * scale
-
+        sums.append(((total + total.T) * scale).reshape(ngx * ngy, 8, cols))
+    low_rows = lax.broadcasted_iota(jnp.int32, (ngx * ngy, 8, cols), 1) < 4
+    turned = [pltpu.roll(part, 4, 1) for part in sums]
+    shape = (2, 4, 4, 8, cols)
+    core, zl = lax.rem(gx, 2), gx // 2
+    first = jnp.where(low_rows, sums[0], turned[1]).reshape((2,) + shape)
+    second = jnp.where(low_rows, turned[0], sums[1]).reshape((2,) + shape)
+    for c in range(2):
+        q[:, c, :, :, 0] = first[:, c]
+        q[:, c, :, :, 1] = second[:, c]
+    place = {"x": gy // 4, "y": lax.rem(gy, 4), "z": gz * 2 + zl}
+
+    def device_of(dim, at):
+        x, y, z = (at if dim == d else place[d] for d in "xyz")
+        return (lax.rem(z, 2) * 2 + core, x * 4 + y, z // 2)
+
+    pending = []
+
+    def send(source, target, sem, device):
+        copy = pltpu.make_async_remote_copy(
+            src_ref=source, dst_ref=target, send_sem=rsend.at[sem], recv_sem=rrecv.at[sem],
+            device_id=device, device_id_type=MESH,
+        )
+        copy.start()
+        pending.append(copy)
+        return copy
+
+    def pick(buf, dims, dim, at):
+        index = []
+        for d in dims:
+            hit = {"l": lax.rem(at, 2), "h": at // 2}.get(d) if dim == "z" else at if d == dim else None
+            index.append(slice(None) if hit is None else hit)
+        return tuple(index)
+
+    swaps = []
+    for t in range(tiles):
+        lanes = slice(t * 128, (t + 1) * 128)
+        swaps.append(
+            send(
+                q.at[:, 1 - core, :, :, :, :, lanes], stage[0][t], t,
+                (zl * 2 + 1 - core, gy, gz),
+            )
+        )
+    held = []
+    for t in range(tiles):
+        lanes = slice(t * 128, (t + 1) * 128)
+        swaps[t].wait_recv()
+        stage[0][t][...] += q[:, core, :, :, :, :, lanes]
+        held.append((stage[0][t], "lxyh"))
+        held[t] = (held[t], exchange_start(t, 0, held[t], pick, place, device_of, send, stage))
+    for s in range(3):
+        for t in range(tiles):
+            (buf, dims), copies_t = held[t]
+            dim = ORDERS[t][s]
+            total = buf[pick(buf, dims, dim, place[dim])]
+            for j, copy in enumerate(copies_t):
+                copy.wait_recv()
+                total = total + stage[s + 1][t][j]
+            if s == 2:
+                stiff_ref[:, t * 128 : (t + 1) * 128] = total[:4]
+                mass_ref[:, t * 128 : (t + 1) * 128] = total[4:]
+                continue
+            left = "".join(d for d in dims if d not in GONE[dim])
+            kept = keep[s][t]
+            kept[...] = total
+            held[t] = ((kept, left), None)
+            held[t] = (held[t][0], exchange_start(t, s + 1, held[t][0], pick, place, device_of, send, stage))
+    for copy in pending:
+        copy.wait_send()
     for k, link in enumerate(links):
         @pl.when(sends_if(link))
         def _(k=k):
@@ -345,6 +462,7 @@
         ],
         axis=0,
     )
+    shapes, keeps = stage_shapes()
     anyspace = pl.BlockSpec(memory_space=pl.ANY)
     vmem = pl.BlockSpec(memory_space=pltpu.VMEM)
     kernel = lambda *refs: local_kernel(
@@ -352,9 +470,9 @@
     )
     return pl.pallas_call(
         kernel,
-        out_shape=jax.ShapeDtypeStruct((cols, 2 * cols), F32),
+        out_shape=[jax.ShapeDtypeStruct((4, cols), F32)] * 2,
         in_specs=[anyspace] + [vmem] * 8,
-        out_specs=vmem,
+        out_specs=[vmem] * 2,
         scratch_shapes=[
             pltpu.VMEM((nx, ny, nz, cols), BF16),
             pltpu.VMEM((nx // 2, cols, 2 * n), BF16),
@@ -368,7 +486,11 @@
             pltpu.SemaphoreType.DMA((nx,)),
             pltpu.SemaphoreType.DMA((26,)),
             pltpu.SemaphoreType.DMA((26,)),
-        ],
+            pltpu.VMEM((2, 2, 4, 4, 2, 8, cols), F32),
+            pltpu.SemaphoreType.DMA((10 * tiles,)),
+            pltpu.SemaphoreType.DMA((10 * tiles,)),
+        ]
+        + [pltpu.VMEM(x, F32) for row in shapes + keeps for x in row],
         compiler_params=pltpu.CompilerParams(
             collective_id=0, has_side_effects=True, vmem_limit_bytes=63 * 1024 * 1024
         ),
@@ -376,23 +498,8 @@
     )(eigvecs, flat, faces, zf, zx, plane, wy, wx, wz)
 
 
-def split_up(x, dim, devices):
-    dims = x.shape
-    parts = x.reshape(*dims[:dim], devices, dims[dim] // devices, *dims[dim + 1 :])
-    return jnp.moveaxis(parts, dim, 0)
-
-
-def sum_at_owner(x, axis, dim):
-    devices = lax.axis_size(axis)
-    parts = lax.all_to_all(split_up(x, dim, devices), axis, 0, 0, tiled=True)
-    return jnp.sum(parts, axis=0)
-
-
 def per_device(eigvecs, material):
-    columns = eigvecs.shape[3]
-    part = local_sums(eigvecs, material)
-    summed = sum_at_owner(sum_at_owner(sum_at_owner(part, "gx", 0), "gy", 0), "gz", 0)
-    return summed[:, :columns], summed[:, columns:]
+    return tuple(local_sums(eigvecs, material))
 
 
 def solution(mesh):

time: 110 us -> 76.1 us (0.69)
  blocking collectives: 57.1 us -> 0 us
  Pallas kernels: 42.3 us -> 63.8 us
  local copies, waits for them, and re-layouts: 8.63 us -> 10.6 us
    all_to_all x3 -> x0, blocking collectives: 57.1 us -> none  [sum_at_owner(): parts = lax.all_to_all(split_up(x, dim, devices), axis, 0, 0, tiled=True)]
    pallas_call x1, Pallas kernels: 42.3 us -> 63.8 us  [local_sums(): pl.pallas_call(kernel, out_shape=[jax.ShapeDtypeStruct((4, cols), F32)] *...]
    unnamed x3 -> x5, local copies, waits for them, and re-layouts: 0.28 us -> 2.87 us
where the time goes in v2:
time: 76.1 us; the launch traced here: 75.7 us
  Pallas kernels  63.8 us (84%)
  local copies, waits for them, and re-layouts  10.6 us (14%)
    pallas_call x1, Pallas kernels, local_sums(): pl.pallas_call(kernel, out_shape=[jax.ShapeDtypeStruct((4, cols), F32)] *...  63.8 us
    unnamed x5, local copies, waits for them, and re-layouts  2.87 us
    reshape x1, local copies, waits for them, and re-layouts, local_sums(): flat = material.reshape(2, nx, n)  1.62 us
    dynamic_slice x1, local copies, waits for them, and re-layouts, local_sums(): zface = lax.dynamic_index_in_dim(eigvecs, at, 2, False)  1.53 us

profile of v2, /device:TPU:0, one launch (start us, length us, event | category | flops | bytes accessed | tf_op | source)
XLA Modules:
  0.0 75.7 jit_solution(9015808049507460746)
XLA Ops:
  0.6 1.0 %constant_dynamic-slice_fusion.1 = f32[2,16,8,1]{3,2,1,0:T(8,128)S(1)} fusion(f32[2,16,8,48]{3,2,1,0:T(8,128)} %param.7, s32[]{:T(128)S(6)} %select_n.8), kind=kLoop, calls=%fused_computation.11 | loop fusion | bytes 2052 | tf_op jit(solution)/shard_map/jit(dynamic_index_in_dim)/dynamic_slice | solution.py:447
  1.6 0.2 copy.14
  1.8 0.1 slice.14
  1.9 0.1 copy.16
  2.0 0.1 reshape.15
  2.1 0.1 reshape.14
  2.2 1.0 %slice_reduce_fusion = f32[2,16,48]{2,1,0:T(8,128)S(1)} fusion(f32[2,16,8,48]{3,2,1,0:T(8,128)} %param.7), kind=kLoop, calls=%fused_computation.8 | loop fusion | bytes 12288 | tf_op jit(solution)/shard_map/slice | solution.py:458
  3.1 0.1 reshape_squeeze.6
  3.2 0.7 slice.13
  3.9 0.1 reshape_squeeze.7
  4.0 0.1 pad.23.clone
  4.1 0.7 fusion.1.refs_2_
  4.8 1.5 %constant_dynamic-slice_fusion = bf16[16,8,1,512]{3,2,1,0:T(2,128)(2,1)S(1)} fusion(bf16[16,8,48,512]{3,2,1,0:T(8,128)(2,1)} %refs_0_.1, s32[]{:T(128)S(6)} %select_n.8), kind=kLoop, calls=%fused_computation.10 | loop fusion | bytes 262148 | tf_op jit(solution)/shard_map/jit(dynamic_index_in_dim)/dynamic_slice | solution.py:444
  6.3 0.6 pad.19.refs_4_
  7.0 0.8 %copy.20 = bf16[16,8,1,512]{3,0,1,2:T(8,128)(2,1)} copy(bf16[16,8,1,512]{3,2,1,0:T(2,128)(2,1)S(1)} %constant_dynamic-slice_fusion) | data formatting | bytes 262144 | tf_op jit(solution)/shard_map/jit(dynamic_index_in_dim)/squeeze | solution.py:444
  7.7 1.6 %reshape.13.refs_1_ = f32[2,16,384]{2,1,0:T(8,128)} reshape(f32[2,16,8,48]{3,2,1,0:T(8,128)} %param.7) | data formatting | bytes 98304 | tf_op jit(solution)/shard_map/reshape | solution.py:448
  9.4 63.8 %local_sums.1 = (f32[4,512]{1,0:T(4,128)}, f32[4,512]{1,0:T(4,128)}) custom-call(bf16[16,8,48,512]{3,2,1,0:T(8,128)(2,1)} %refs_0_.1, f32[2,16,384]{2,1,0:T(8,128)} %reshape.13.refs_1_, f32[8,768]{1,0:T(8,128)} %fusion.1.refs_2_, bf16[8,16,512]{2,1,0:T(8,128)(2,1)} %bitcast.15, bf16[2,16,512]{2,1,0:T(8,128)(2,1)} %pad.19.refs_4_, ...), custom_call_target="tpu_custom_call" | custom-call | tf_op jit(solution)/shard_map/local_sums/pallas_call | solution.py:471
  73.1 1.3 %copy.24 = f32[4,512]{1,0:T(4,128)} copy(f32[4,512]{1,0:T(4,128)} %get-tuple-element.4) | data formatting | bytes 16384
  74.4 1.3 %copy.25 = f32[4,512]{1,0:T(4,128)} copy(f32[4,512]{1,0:T(4,128)} %get-tuple-element.5) | data formatting | bytes 16384
  (5 shorter events, 0.1 us)

commit v3 on v2

v3 whole, which is shorter than its diff:
```python
import jax
import jax.numpy as jnp
import numpy as np
from jax import lax
from jax.experimental import pallas as pl
from jax.experimental.pallas import tpu as pltpu
from jax.sharding import PartitionSpec as P

MESH = pl.DeviceIdType.MESH
F32, BF16 = jnp.float32, jnp.bfloat16
PC, PM = 1.0 / 16.0, 1.0 / 216.0


def taps(rows, cols, middle):
    gap = np.abs(rows[:, None] - cols[None, :])
    return np.where(gap == 0, middle, np.where(gap == 1, 1, 0))


def pair_weights(halo, own, middle):
    total = 1
    for h, o in zip(halo, own):
        total = total * taps(h, o, middle)
    return total


def grid(*axes):
    return [a.reshape(-1) for a in np.meshgrid(*axes, indexing="ij")]


def stacked(halo, own, pad):
    w = np.concatenate([pair_weights(halo, own, 2), pair_weights(halo, own, 4)], axis=1)
    w = np.concatenate([w, np.zeros((pad, w.shape[1]), w.dtype)], axis=0)
    return w.astype(np.float32)


WINDOWS = ((0, 256), (0, 384), (128, 384))
YWINDOWS = ((0, 256), (128, 384), (256, 512))
ZWINDOWS = ((0, 256),)


def banded(w, windows):
    m = w.shape[1] // 2
    found = []
    for t, (lo, hi) in enumerate(windows):
        own = np.r_[t * 128 : (t + 1) * 128, m + t * 128 : m + (t + 1) * 128]
        outside = np.delete(w[:, own], np.s_[lo:hi], axis=0)
        assert not outside.any()
        found.append(w[lo:hi][:, own])
    return np.concatenate(found)


def weight_arrays(nx, ny, nz):
    hx = nx // 2
    y, z = grid(np.arange(ny), np.arange(nz))
    plane = banded(stacked([y, z], [y, z], 0), WINDOWS)
    hxx, hzz = grid(np.arange(-1, hx + 1), np.arange(nz))
    oxx, ozz = grid(np.arange(hx), np.arange(nz))
    wy = stacked([hxx, hzz, 0 * hxx + 1], [oxx, ozz, 0 * oxx], 16)
    wy = banded(np.concatenate([np.zeros((16, wy.shape[1]), np.float32), wy]), YWINDOWS)
    far = 99
    slabs = []
    xs = np.arange(nx)
    for yy in range(ny):
        slabs.append((xs, 0 * xs + yy))
    ys = np.concatenate([np.arange(ny), far + 0 * np.arange(nx - ny)])
    first = np.where(xs == 0, 0, far)
    last = np.where(xs == nx - 1, 0, far)
    slabs += [(xs, 0 * xs - 1), (xs, 0 * xs + ny)]
    slabs += [(0 * xs - 1, ys), (0 * xs + nx, ys)]
    slabs += [(last - 1, 0 * xs - 1), (last - 1, 0 * xs + ny)]
    slabs += [(first + nx, 0 * xs - 1), (first + nx, 0 * xs + ny)]
    zx = np.concatenate([s[0] for s in slabs])
    zy = np.concatenate([s[1] for s in slabs])
    oyy, oxx = grid(np.arange(ny), np.arange(nx))
    wz = banded(stacked([zx, zy, 0 * zx + 1], [oxx, oyy, 0 * oxx], 0), ZWINDOWS)
    return plane, wy, wz


def nt(a, b):
    return lax.dot_general(a, b, (((1,), (1,)), ((), ())), preferred_element_type=F32)


def nn(a, b):
    return jnp.dot(a, b, preferred_element_type=F32)


def split(x):
    pad = jnp.zeros(((-x.shape[0]) % 16, x.shape[1]), F32)
    x = jnp.concatenate([x, pad], axis=0) if pad.shape[0] else x
    high = x.astype(BF16)
    rest = x - high.astype(F32)
    mid = rest.astype(BF16)
    low = (rest - mid.astype(F32)).astype(BF16)
    return jnp.concatenate([high, mid, low], axis=0)


def joined(x, rows):
    return (x[:rows] + x[16 : 16 + rows]) + x[32 : 32 + rows]


def exact(a, b):
    return joined(nn(split(a), b), a.shape[0])


def exact_nt(a, b):
    return joined(nt(split(a), b), a.shape[0])


ORDERS = ("yxz", "xzy", "zyx", "xyz")
GONE = {"x": "x", "y": "y", "z": "lh"}
SIZE = {"l": 2, "h": 2, "x": 4, "y": 4}
tiles = len(ORDERS)


def exchange_start(t, s, held, pick, place, device_of, send, stage):
    buf, dims = held
    dim = ORDERS[t][s]
    copies = []
    for j in range(3):
        at = lax.rem(place[dim] + j + 1, 4)
        copies.append(
            send(
                buf.at[pick(buf, dims, dim, at)], stage[s + 1][t].at[j],
                tiles + (s * tiles + t) * 3 + j, device_of(dim, at),
            )
        )
    return copies


def partners(gx, gy, gz):
    core, z = lax.rem(gx, 2), gz * 2 + gx // 2
    x, y = gy // 4, lax.rem(gy, 4)
    found = [(gx + 1 - 2 * core, gy, gz)]
    for j in range(1, 4):
        found.append((gx, x * 4 + lax.rem(y + j, 4), gz))
        found.append((gx, lax.rem(x + j, 4) * 4 + y, gz))
        zz = lax.rem(z + j, 4)
        found.append((lax.rem(zz, 2) * 2 + core, gy, zz // 2))
    return found


def stage_shapes():
    shapes, keeps = [[(2, 4, 4, 2, 8, 128)] * tiles], []
    for s in range(3):
        row, kept = [], []
        for t in range(tiles):
            gone = "".join(GONE[d] for d in ORDERS[t][: s + 1])
            left = tuple(SIZE[d] for d in "lxyh" if d not in gone) + (8, 128)
            row.append((3,) + left)
            kept.append(left)
        shapes.append(row)
        keeps.append(kept)
    return shapes, keeps[:2]


def local_kernel(
    dims, scale,
    v_ref, mat_ref, wp_any, wy_any, wz_any,
    out_ref,
    vbuf, vt, fbuf, ym, acc, hy, hx, hz, fh, vsem, send_sem, recv_sem,
    q, rsend, rrecv, faces_ref, zf_ref, zx_ref, wp_ref, wy_ref, wz_ref, wsem,
    ys, ht, hfar, owned, us, um, *rest,
):
    stage = [rest[s * tiles : (s + 1) * tiles] for s in range(4)]
    keep = [rest[(4 + s) * tiles : (5 + s) * tiles] for s in range(2)]
    nx, ny, nz, cols, ngx, ngy = dims
    n = ny * nz
    gx, gy, gz = lax.axis_index("gx"), lax.axis_index("gy"), lax.axis_index("gz")
    hx_n = nx // 2

    loads = [pltpu.make_async_copy(v_ref.at[x], vbuf.at[x], vsem.at[x]) for x in range(nx)]
    weights = [
        pltpu.make_async_copy(a, b, wsem.at[k])
        for k, (a, b) in enumerate(((wp_any, wp_ref), (wy_any, wy_ref), (wz_any, wz_ref)))
    ]
    weights[0].start()
    for load in loads:
        load.start()
    for load in weights[1:]:
        load.start()

    def zrow(k):
        return hz.at[k]

    links = [
        ((0, 1), False, v_ref.at[:, ny - 1], hy.at[pl.ds(1, nx)]),
        ((1, 1), False, v_ref.at[nx - 1, ny - 1], hy.at[0]),
        ((-1, 1), False, v_ref.at[0, ny - 1], hy.at[nx + 1]),
        ((1, 0), False, v_ref.at[nx - 1], hx),
        ((0, 0), True, zf_ref, hz.at[pl.ds(0, ny)]),
        ((0, 1), True, zf_ref.at[ny - 1], zrow(ny)),
        ((0, -1), True, zf_ref.at[0], zrow(ny + 1)),
        ((1, 0), True, zx_ref.at[1], zrow(ny + 2)),
        ((-1, 0), True, zx_ref.at[0], zrow(ny + 3)),
        ((1, 1), True, zf_ref.at[ny - 1], zrow(ny + 4)),
        ((1, -1), True, zf_ref.at[0], zrow(ny + 5)),
        ((-1, 1), True, zf_ref.at[ny - 1], zrow(ny + 6)),
        ((-1, -1), True, zf_ref.at[0], zrow(ny + 7)),
    ]

    def inside(dx, dy):
        ok = None
        for move, at, count in ((dx, gx, ngx), (dy, gy, ngy)):
            here = None
            if move == 1:
                here = at < count - 1
            if move == -1:
                here = at > 0
            if here is not None:
                ok = here if ok is None else jnp.logical_and(ok, here)
        return ok

    def both(a, b):
        return b if a is None else jnp.logical_and(a, b)

    def sends_if(link):
        (dx, dy), cut, _, _ = link
        ok = inside(dx, dy)
        return both(ok, gz == 0) if cut else ok

    def gets_if(link):
        (dx, dy), cut, _, _ = link
        ok = inside(-dx, -dy)
        return both(ok, gz == 1) if cut else ok

    hy[...] = jnp.zeros_like(hy)
    hx[...] = jnp.zeros_like(hx)
    hz[...] = jnp.zeros_like(hz)
    fh[...] = jnp.zeros_like(fh)

    barrier = pltpu.get_barrier_semaphore()
    targets = 0
    for link in links:
        (dx, dy), cut, _, _ = link
        source = (gx - dx, gy - dy, 0 if cut else gz)

        @pl.when(gets_if(link))
        def _(source=source):
            pl.semaphore_signal(barrier, inc=1, device_id=source, device_id_type=MESH)

        targets = targets + sends_if(link).astype(jnp.int32)
    for device in partners(gx, gy, gz):
        pl.semaphore_signal(barrier, inc=1, device_id=device, device_id_type=MESH)
    pl.semaphore_wait(barrier, targets + 10)

    copies = []
    for k, link in enumerate(links):
        (dx, dy), cut, source, target = link
        device = (gx + dx, gy + dy, 1 if cut else gz)
        pair = [
            pltpu.make_async_remote_copy(
                src_ref=s, dst_ref=t, send_sem=send_sem.at[2 * k + j],
                recv_sem=recv_sem.at[2 * k + j], device_id=device, device_id_type=MESH,
            )
            for j, (s, t) in enumerate(((faces_ref, fh.at[k]), (source, target)))
        ]
        copies.append(pair)
        if not cut:

            @pl.when(sends_if(link))
            def _(pair=pair):
                pair[1].start()

    kappa, rho = (
        jnp.concatenate([mat_ref[j, :, y, :] for y in range(ny)], axis=1) for j in range(2)
    )
    at_low = gz == 1
    cell = lax.broadcasted_iota(jnp.int32, (n, 128), 0)
    lane = lax.broadcasted_iota(jnp.int32, (n, 128), 1)
    edge_z = jnp.where(at_low, 0, nz - 1)
    hot = jnp.logical_and(cell == lane * nz + edge_z, lane < ny).astype(F32).astype(BF16)
    width = nx * nz
    for j, rows in enumerate((kappa, rho)):
        faces_ref[j : j + 1, :] = jnp.concatenate(
            [rows[x : x + 1, (ny - 1) * nz :] for x in range(nx)], axis=1
        )
        faces_ref[2 + j : 3 + j, :] = jnp.concatenate(
            [rows[nx - 1 :], jnp.zeros((1, width - n), F32)], axis=1
        )
        edge_rows = exact(rows, hot)
        turned = jnp.concatenate([edge_rows, jnp.zeros((128 - nx, 128), F32)], axis=0).T
        faces_ref[4 + j : 5 + j, :] = jnp.concatenate(
            [turned[y : y + 1, :nx] for y in range(ny)]
            + [edge_rows[:1, :nx], edge_rows[nx - 1 :, :nx]]
            + [jnp.zeros((1, width - (ny + 2) * nx), F32)],
            axis=1,
        )
    faces_ref[6:8, :] = jnp.zeros((2, width), F32)

    def z_edge(x, y, count):
        tall, low = vbuf[x, y, nz - 16 :, :], vbuf[x, y, :16, :]
        picked = jnp.where(at_low, low.astype(F32)[:, 0, :], tall.astype(F32)[:, 15, :])
        return picked.astype(BF16)

    def later_sends():
        for y in range(ny):
            zf_ref[y] = z_edge(slice(None), y, nx)
        zx_ref[...] = jnp.zeros_like(zx_ref)
        for j, x in enumerate((0, nx - 1)):
            zx_ref[j, :ny] = z_edge(x, slice(None), ny)
        for link, pair in zip(links, copies):

            @pl.when(sends_if(link))
            def _(link=link, pair=pair):
                pair[0].start()
                if link[1]:
                    pair[1].start()

    weights[0].wait()
    starts = np.cumsum([0] + [hi - lo for lo, hi in WINDOWS])
    zero = jnp.zeros((1, n), F32)
    filtered = jnp.concatenate(
        [
            exact(kappa[:, lo:hi], wp_ref[starts[t] : starts[t + 1], :128])
            for t, (lo, hi) in enumerate(WINDOWS)
        ],
        axis=1,
    )
    around = (
        jnp.concatenate([zero, filtered[:-1]], axis=0)
        + 2.0 * filtered
        + jnp.concatenate([filtered[1:], zero], axis=0)
    )
    diag = 0.5 * (3.5 * kappa + PC * around - 0.5 * kappa)
    coef_v = diag + 0.5 * kappa
    coef_s = PC * kappa
    coef_m = PM * rho

    def load_plane(x):
        if x < nx:
            vt[x // 2, :, (x % 2) * n : (x % 2 + 1) * n] = vbuf[x].reshape(n, cols).T

    def stage_a(x):
        if x < nx:
            load_plane(x)
            for t, (lo, hi) in enumerate(WINDOWS):
                base = (x % 2) * n
                fbuf[x % 6, :, t * 256 : (t + 1) * 256] = nn(
                    vt[x // 2, :, base + lo : base + hi], wp_ref[starts[t] : starts[t + 1]]
                )

    chunk = 32

    def stage_b(x, lo, hi):
        half = (x % 2) * n
        buf = (x // 2) % 2
        for r in range(lo, hi, chunk):
            rows = slice(r, r + chunk)
            for t in range(n // 128):
                cv, cs, cm = (
                    c[x : x + 1, t * 128 : (t + 1) * 128] for c in (coef_v, coef_s, coef_m)
                )
                at_s = slice(t * 256, t * 256 + 128)
                at_m = slice(t * 256 + 128, (t + 1) * 256)
                at_v = slice(half + t * 128, half + (t + 1) * 128)
                s = 2.0 * fbuf[x % 6, rows, at_s]
                m = 4.0 * fbuf[x % 6, rows, at_m]
                for near in (x - 1, x + 1):
                    if 0 <= near < nx:
                        s = s + fbuf[near % 6, rows, at_s]
                        m = m + fbuf[near % 6, rows, at_m]
                v = vt[x // 2, rows, at_v].astype(F32)
                ys[x // 2, rows, at_v] = (cv * v - cs * s).astype(BF16)
                ym[buf, rows, at_v] = (cm * m).astype(BF16)

    def stage_c(pair):
        if pair < 0:
            return
        part = nt(vt[pair], ym[pair % 2])
        if pair == 0:
            acc[1] = part
        else:
            acc[1] += part

    pairs = nx // 2
    for load in loads:
        load.wait()
    for x in range(3):
        stage_a(x)
    for i in range(pairs):
        for x in range(2):
            stage_a(2 * i + 3 + x)
            stage_b(2 * i + x, 0, cols)
        stage_c(i - 1)
        if i == 0:
            later_sends()
    stage_c(pairs - 1)
    for load in weights[1:]:
        load.wait()

    for k, link in enumerate(links):
        @pl.when(gets_if(link))
        def _(k=k):
            for copy in copies[k]:
                copy.wait_recv()

    def row(k, r, lo, hi):
        return fh[k, r : r + 1, lo:hi]

    def wide(x):
        return jnp.concatenate(x, axis=1)

    used = (hx_n + 2) * nz
    blank = jnp.zeros((1, 16), F32)
    edge = (nx - 1) * nz

    def group(k_at, m_at, halo, kh, rh, own, ko, ro, w_ref, windows):
        k, m = halo.shape[0], own.shape[1]
        ht[:, k_at : k_at + k] = halo.T
        owned[:, m_at : m_at + m] = own
        kc, rc = (jnp.broadcast_to(r, (128, k)).T for r in (kh, rh))
        far = jnp.zeros((1, k), F32)
        first = 0
        for t, (lo, hi) in enumerate(windows):
            tile = w_ref[first : first + hi - lo]
            first += hi - lo
            lanes = slice(t * 128, (t + 1) * 128)
            wc, wm = tile[:, :128].astype(F32), tile[:, 128:].astype(F32)
            ls = (wc * ((-PC) * (kc[lo:hi] + ko[:, lanes]))).astype(BF16)
            lm = (wm * (PM * (rc[lo:hi] + ro[:, lanes]))).astype(BF16)
            fbuf[t, :, :256] = nn(
                ht[:, k_at + lo : k_at + hi], jnp.concatenate([ls, lm], axis=1)
            )
            own_diag = (0.5 * PC) * jnp.sum(wc * kc[lo:hi], axis=0, keepdims=True)
            part = (0.5 * PC) * exact_nt(ko[:, lanes], tile[:, :128])
            sides = [jnp.zeros((1, lo), F32), part, jnp.zeros((1, k - hi), F32)]
            far = far + wide([x for x in sides if x.shape[1]])
            at = slice(m_at + t * 128, m_at + (t + 1) * 128)
            for r in range(0, cols, 64):
                rows = slice(r, r + 64)
                us[rows, at] = (
                    own_diag * owned[rows, at].astype(F32) + fbuf[t, rows, :128]
                ).astype(BF16)
                um[rows, at] = fbuf[t, rows, 128:256].astype(BF16)
        for r in range(0, cols, 32):
            rows = slice(r, r + 32)
            at = slice(k_at, k_at + k)
            hfar[rows, at] = (far * ht[rows, at].astype(F32)).astype(BF16)

    ky = 2 * 16 + used
    for side in range(2):
        if side == 0:
            pick = lambda r: wide(
                [blank, row(1, r, edge, edge + nz), row(0, r, 0, used - nz), blank]
            )
        else:
            pick = lambda r: wide(
                [blank, row(0, r, (hx_n - 1) * nz, nx * nz), row(2, r, 0, nz), blank]
            )
        start = side * hx_n
        none = jnp.zeros((16, cols), BF16)
        halo = jnp.concatenate(
            [none, hy[start : start + hx_n + 2].reshape(used, cols), none], axis=0
        )
        own = vbuf[start : start + hx_n, 0].reshape(hx_n * nz, cols).T
        mine = [
            wide([rows[x : x + 1, :nz] for x in range(start, start + hx_n)])
            for rows in (kappa, rho)
        ]
        group(side * ky, side * n, halo, pick(0), pick(1), own, mine[0], mine[1], wy_ref, YWINDOWS)

    group(
        2 * ky, 2 * n, hx[...].reshape(n, cols), row(3, 2, 0, n), row(3, 3, 0, n),
        vt[0, :, :n], kappa[:1], rho[:1], wp_ref, WINDOWS,
    )

    nf = nx * ny
    low, high = (nf - nx, nf), (0, nx)

    def zpick(r):
        spans = [(4, (0, nf)), (5, low), (6, high), (7, (nf + nx, nf + 2 * nx)),
                 (8, (nf, nf + nx)), (9, low), (10, high), (11, low), (12, high)]
        return wide([row(k, r, lo, hi) for k, (lo, hi) in spans])

    group(
        2 * ky + n, 3 * n, hz[...].reshape((ny + 8) * nx, cols), zpick(4), zpick(5),
        zf_ref[...].reshape(nf, cols).T, faces_ref[4:5, :nf], faces_ref[5:6, :nf],
        wz_ref, ZWINDOWS,
    )

    core, zl = lax.rem(gx, 2), gx // 2
    place = {"x": gy // 4, "y": lax.rem(gy, 4), "z": gz * 2 + zl}

    def device_of(dim, at):
        x, y, z = (at if dim == d else place[d] for d in "xyz")
        return (lax.rem(z, 2) * 2 + core, x * 4 + y, z // 2)

    pending = []

    def send(source, target, sem, device):
        copy = pltpu.make_async_remote_copy(
            src_ref=source, dst_ref=target, send_sem=rsend.at[sem], recv_sem=rrecv.at[sem],
            device_id=device, device_id_type=MESH,
        )
        copy.start()
        pending.append(copy)
        return copy

    def pick_part(buf, dims, dim, at):
        index = []
        for d in dims:
            hit = {"l": lax.rem(at, 2), "h": at // 2}.get(d) if dim == "z" else at if d == dim else None
            index.append(slice(None) if hit is None else hit)
        return tuple(index)

    half = cols // 2
    low_rows = lax.broadcasted_iota(jnp.int32, (16, 8, half), 1) < 4

    def symmetrize(h):
        for b in range(4):
            block = slice(b * 128, (b + 1) * 128)
            total = (acc[h, block] + acc[h, :, block].T) * scale
            left, right = total[:, :half].reshape(16, 8, half), total[:, half:].reshape(16, 8, half)
            first = jnp.where(low_rows, left, pltpu.roll(right, 4, 1))
            second = jnp.where(low_rows, pltpu.roll(left, 4, 1), right)
            q[h, b // 2, b % 2, :, :, 0] = first.reshape(4, 4, 8, half)
            q[h, b // 2, b % 2, :, :, 1] = second.reshape(4, 4, 8, half)

    matrix = (1, 1, 0, 0)
    held = [None] * tiles

    def swap(t):
        lanes = slice((t % 2) * 128, (t % 2 + 1) * 128)
        held[t] = send(
            q.at[matrix[t], :, 1 - core, :, :, :, :, lanes], stage[0][t], t,
            (zl * 2 + 1 - core, gy, gz),
        )

    def swapped(t):
        lanes = slice((t % 2) * 128, (t % 2 + 1) * 128)
        held[t].wait_recv()
        stage[0][t][...] += q[matrix[t], :, core, :, :, :, :, lanes]
        buf = (stage[0][t], "lxyh")
        held[t] = (buf, exchange_start(t, 0, buf, pick_part, place, device_of, send, stage))

    def advance(t, s):
        (buf, dims), copies_t = held[t]
        dim = ORDERS[t][s]
        total = buf[pick_part(buf, dims, dim, place[dim])]
        for j, copy in enumerate(copies_t):
            copy.wait_recv()
            total = total + stage[s + 1][t][j]
        if s == 2:
            rows = slice(4 * matrix[t], 4 * matrix[t] + 4)
            out_ref[rows, (t % 2) * 128 : (t % 2 + 1) * 128] = total[:4]
            out_ref[rows, half + (t % 2) * 128 : half + (t % 2 + 1) * 128] = total[4:]
            return
        kept = keep[s][t]
        kept[...] = total
        buf = (kept, "".join(d for d in dims if d not in GONE[dim]))
        held[t] = (buf, exchange_start(t, s + 1, buf, pick_part, place, device_of, send, stage))

    acc[1] += nt(owned[...], um[...])
    symmetrize(1)
    swap(0)
    swap(1)
    acc[0] = nt(owned[...], us[...])
    acc[0] += nt(ht[...], hfar[...])
    for pair in range(pairs):
        acc[0] += nt(vt[pair], ys[pair])
        if pair == 1:
            swapped(0)
            swapped(1)
    symmetrize(0)
    swap(2)
    swap(3)
    swapped(2)
    swapped(3)
    for s in range(3):
        for t in range(tiles):
            advance(t, s)
    for copy in pending:
        copy.wait_send()
    for k, link in enumerate(links):
        @pl.when(sends_if(link))
        def _(k=k):
            for copy in copies[k]:
                copy.wait_send()


def local_sums(eigvecs, material):
    nx, ny, nz, cols = eigvecs.shape
    n = ny * nz
    count = {a: lax.axis_size(a) for a in ("gx", "gy", "gz")}
    cells = nx * ny * nz * count["gx"] * count["gy"] * count["gz"]
    plane, wy, wz = (jnp.asarray(w, BF16) for w in weight_arrays(nx, ny, nz))
    width = nx * nz
    shapes, keeps = stage_shapes()
    own_cells = 3 * n + nx * ny
    halo_cells = 2 * (32 + (nx // 2 + 2) * nz) + n + (ny + 8) * nx
    anyspace = pl.BlockSpec(memory_space=pl.ANY)
    vmem = pl.BlockSpec(memory_space=pltpu.VMEM)
    kernel = lambda *refs: local_kernel(
        (nx, ny, nz, cols, count["gx"], count["gy"]), 0.5 / cells, *refs
    )
    return pl.pallas_call(
        kernel,
        out_shape=jax.ShapeDtypeStruct((8, cols), F32),
        in_specs=[anyspace, vmem] + [anyspace] * 3,
        out_specs=vmem,
        scratch_shapes=[
            pltpu.VMEM((nx, ny, nz, cols), BF16),
            pltpu.VMEM((nx // 2, cols, 2 * n), BF16),
            pltpu.VMEM((6, cols, 2 * n), F32),
            pltpu.VMEM((2, cols, 2 * n), BF16),
            pltpu.VMEM((2, cols, cols), F32),
            pltpu.VMEM((nx + 3, nz, cols), BF16),
            pltpu.VMEM((ny, nz, cols), BF16),
            pltpu.VMEM((ny + 8, nx, cols), BF16),
            pltpu.VMEM((13, 8, width), F32),
            pltpu.SemaphoreType.DMA((nx,)),
            pltpu.SemaphoreType.DMA((26,)),
            pltpu.SemaphoreType.DMA((26,)),
            pltpu.VMEM((2, 2, 2, 4, 4, 2, 8, cols // 2), F32),
            pltpu.SemaphoreType.DMA((10 * tiles,)),
            pltpu.SemaphoreType.DMA((10 * tiles,)),
            pltpu.VMEM((8, width), F32),
            pltpu.VMEM((ny, nx, cols), BF16),
            pltpu.VMEM((2, nx, cols), BF16),
            pltpu.VMEM(plane.shape, BF16),
            pltpu.VMEM(wy.shape, BF16),
            pltpu.VMEM(wz.shape, BF16),
            pltpu.SemaphoreType.DMA((3,)),
            pltpu.VMEM((nx // 2, cols, 2 * n), BF16),
            pltpu.VMEM((cols, halo_cells), BF16),
            pltpu.VMEM((cols, halo_cells), BF16),
        ]
        + [pltpu.VMEM((cols, own_cells), BF16)] * 3
        + [pltpu.VMEM(x, F32) for row in shapes + keeps for x in row],
        compiler_params=pltpu.CompilerParams(
            collective_id=0, has_side_effects=True, vmem_limit_bytes=63 * 1024 * 1024
        ),
        name="local_sums",
    )(eigvecs, material, plane, wy, wz)


def per_device(eigvecs, material):
    both = local_sums(eigvecs, material)
    return both[:4], both[4:]


def solution(mesh):
    return jax.shard_map(
        per_device,
        mesh=mesh,
        in_specs=(P("gx", "gy", "gz", None), P(None, "gx", "gy", "gz")),
        out_specs=(P(("gx", "gy", "gz"), None), P(("gx", "gy", "gz"), None)),
        check_vma=False,
    )
```

time: 76.1 us -> 61.6 us (0.81)
  local copies, waits for them, and re-layouts: 10.6 us -> 1.4 us
  Pallas kernels: 63.8 us -> 59.4 us
    pallas_call x1, Pallas kernels: 63.8 us -> 59.4 us  [local_sums(): pl.pallas_call(kernel, out_shape=jax.ShapeDtypeStruct((8, cols), F32), in...]
    unnamed x5 -> x0, local copies, waits for them, and re-layouts: 2.87 us -> none
    dynamic_slice x2 -> x0, local copies, waits for them, and re-layouts: 2.53 us -> none  [the longest x1 1.53 us: local_sums(): zface = lax.dynamic_index_in_dim(eigvecs, at, 2, False)]
    reshape x3 -> x0, local copies, waits for them, and re-layouts: 1.78 us -> none  [the longest x1 1.62 us: local_sums(): flat = material.reshape(2, nx, n)]
    squeeze x1 -> x0, local copies, waits for them, and re-layouts: 0.78 us -> none  [local_sums(): zface = lax.dynamic_index_in_dim(eigvecs, at, 2, False)]
    slice x4 -> x1, local copies, waits for them, and re-layouts: 1.75 us -> 1.4 us  [per_device(): return (both[:4], both[4:])]
where the time goes in v3:
time: 61.6 us; the launch traced here: 61.4 us
  Pallas kernels  59.4 us (96%)
  local copies, waits for them, and re-layouts  1.4 us (2%)
  between operations  0.64 us (1%)
    pallas_call x1, Pallas kernels, local_sums(): pl.pallas_call(kernel, out_shape=jax.ShapeDtypeStruct((8, cols), F32), in...  59.4 us
    slice x1, local copies, waits for them, and re-layouts, per_device(): return (both[:4], both[4:])  1.4 us

profile of v3, /device:TPU:0, one launch (start us, length us, event | category | flops | bytes accessed | tf_op | source)
XLA Modules:
  0.0 61.4 jit_solution(2138589445808967730)
XLA Ops:
  0.6 59.4 %local_sums.1 = f32[8,512]{1,0:T(8,128)} custom-call(bf16[16,8,48,512]{3,2,1,0:T(8,128)(2,1)} %refs_0_.1, f32[2,16,8,48]{3,2,1,0:T(8,128)} %refs_1_.1, bf16[896,256]{1,0:T(8,128)(2,1)} %constant.6.clone.refs_2_, bf16[768,256]{1,0:T(8,128)(2,1)} %constant.7.clone.refs_3_, bf16[256,256]{1,0:T(8,128)(2,1)} %constant.8.clone.refs_4_), custom_call_target="tpu_custom_call" | custom-call | tf_op jit(solution)/shard_map/local_sums/pallas_call | solution.py:596
  60.0 1.4 %fusion = (f32[4,512]{1,0:T(4,128)}, f32[4,512]{1,0:T(4,128)}) fusion(f32[8,512]{1,0:T(8,128)} %local_sums.1), kind=kLoop, calls=%fused_computation | loop fusion | bytes 32768 | tf_op jit(solution)/shard_map/slice | solution.py:639

commit v4 on v3

--- a/solution.py
+++ b/solution.py
@@ -36,6 +36,9 @@
 WINDOWS = ((0, 256), (0, 384), (128, 384))
 YWINDOWS = ((0, 256), (128, 384), (256, 512))
 ZWINDOWS = ((0, 256),)
+
+
+RELAY = 5
 
 
 def banded(w, windows):
@@ -159,7 +162,7 @@
     out_ref,
     vbuf, vt, fbuf, ym, acc, hy, hx, hz, fh, vsem, send_sem, recv_sem,
     q, rsend, rrecv, faces_ref, zf_ref, zx_ref, wp_ref, wy_ref, wz_ref, wsem,
-    ys, ht, hfar, owned, us, um, *rest,
+    ys, ht, hfar, owned, us, um, hu, hc, hzx, fz_ref, fhz, *rest,
 ):
     stage = [rest[s * tiles : (s + 1) * tiles] for s in range(4)]
     keep = [rest[(4 + s) * tiles : (5 + s) * tiles] for s in range(2)]
@@ -179,23 +182,21 @@
     for load in weights[1:]:
         load.start()
 
-    def zrow(k):
-        return hz.at[k]
-
     links = [
-        ((0, 1), False, v_ref.at[:, ny - 1], hy.at[pl.ds(1, nx)]),
-        ((1, 1), False, v_ref.at[nx - 1, ny - 1], hy.at[0]),
-        ((-1, 1), False, v_ref.at[0, ny - 1], hy.at[nx + 1]),
-        ((1, 0), False, v_ref.at[nx - 1], hx),
-        ((0, 0), True, zf_ref, hz.at[pl.ds(0, ny)]),
-        ((0, 1), True, zf_ref.at[ny - 1], zrow(ny)),
-        ((0, -1), True, zf_ref.at[0], zrow(ny + 1)),
-        ((1, 0), True, zx_ref.at[1], zrow(ny + 2)),
-        ((-1, 0), True, zx_ref.at[0], zrow(ny + 3)),
-        ((1, 1), True, zf_ref.at[ny - 1], zrow(ny + 4)),
-        ((1, -1), True, zf_ref.at[0], zrow(ny + 5)),
-        ((-1, 1), True, zf_ref.at[ny - 1], zrow(ny + 6)),
-        ((-1, -1), True, zf_ref.at[0], zrow(ny + 7)),
+        ((0, 1), 0, v_ref.at[pl.ds(0, hx_n + 1), ny - 1], hy.at[pl.ds(1, hx_n + 1)]),
+        ((1, 1), 0, v_ref.at[nx - 1, ny - 1], hy.at[0]),
+        ((-1, 0), 0, v_ref.at[0, ny - 1], hc),
+        ((1, 0), 0, v_ref.at[nx - 1], hx),
+        ((0, -1), 0, v_ref.at[pl.ds(hx_n, hx_n), 0], hu),
+    ]
+    links = [(o, kind, [(faces_ref, fh.at[k]), (a, b)]) for k, (o, kind, a, b) in enumerate(links)]
+    cut = ((0, 0), 1, [(fz_ref, fhz.at[0]), (zf_ref, hz.at[pl.ds(0, ny)]), (zx_ref, hzx)])
+    relays = [
+        ((0, 1), hz.at[ny - 1]), ((0, -1), hz.at[0]), ((1, 0), hzx.at[1]), ((-1, 0), hzx.at[0]),
+        ((1, 1), hz.at[ny - 1]), ((1, -1), hz.at[0]), ((-1, 1), hz.at[ny - 1]), ((-1, -1), hz.at[0]),
+    ]
+    links = links + [cut] + [
+        (o, 2, [(fhz.at[0], fhz.at[j + 1]), (a, hz.at[ny + j])]) for j, (o, a) in enumerate(relays)
     ]
 
     def inside(dx, dy):
@@ -214,25 +215,29 @@
         return b if a is None else jnp.logical_and(a, b)
 
     def sends_if(link):
-        (dx, dy), cut, _, _ = link
+        (dx, dy), kind, _ = link
         ok = inside(dx, dy)
-        return both(ok, gz == 0) if cut else ok
+        return both(ok, gz == kind - 1) if kind else ok
 
     def gets_if(link):
-        (dx, dy), cut, _, _ = link
+        (dx, dy), kind, _ = link
         ok = inside(-dx, -dy)
-        return both(ok, gz == 1) if cut else ok
+        return both(ok, gz == 1) if kind else ok
 
     hy[...] = jnp.zeros_like(hy)
     hx[...] = jnp.zeros_like(hx)
+    hu[...] = jnp.zeros_like(hu)
+    hc[...] = jnp.zeros_like(hc)
     hz[...] = jnp.zeros_like(hz)
+    hzx[...] = jnp.zeros_like(hzx)
     fh[...] = jnp.zeros_like(fh)
+    fhz[...] = jnp.zeros_like(fhz)
 
     barrier = pltpu.get_barrier_semaphore()
     targets = 0
     for link in links:
-        (dx, dy), cut, _, _ = link
-        source = (gx - dx, gy - dy, 0 if cut else gz)
+        (dx, dy), kind, _ = link
+        source = (gx - dx, gy - dy, 0 if kind == 1 else gz)
 
         @pl.when(gets_if(link))
         def _(source=source):
@@ -241,25 +246,46 @@
         targets = targets + sends_if(link).astype(jnp.int32)
     for device in partners(gx, gy, gz):
         pl.semaphore_signal(barrier, inc=1, device_id=device, device_id_type=MESH)
-    pl.semaphore_wait(barrier, targets + 10)
 
     copies = []
-    for k, link in enumerate(links):
-        (dx, dy), cut, source, target = link
-        device = (gx + dx, gy + dy, 1 if cut else gz)
-        pair = [
-            pltpu.make_async_remote_copy(
-                src_ref=s, dst_ref=t, send_sem=send_sem.at[2 * k + j],
-                recv_sem=recv_sem.at[2 * k + j], device_id=device, device_id_type=MESH,
+    used_sems = 0
+    for (dx, dy), kind, moves in links:
+        device = (gx + dx, gy + dy, 1 if kind == 1 else gz)
+        group_of = []
+        for a, b in moves:
+            group_of.append(
+                pltpu.make_async_remote_copy(
+                    src_ref=a, dst_ref=b, send_sem=send_sem.at[used_sems],
+                    recv_sem=recv_sem.at[used_sems], device_id=device, device_id_type=MESH,
+                )
             )
-            for j, (s, t) in enumerate(((faces_ref, fh.at[k]), (source, target)))
-        ]
-        copies.append(pair)
-        if not cut:
-
-            @pl.when(sends_if(link))
-            def _(pair=pair):
-                pair[1].start()
+            used_sems += 1
+        copies.append(group_of)
+
+    def wait_if(link, k):
+        @pl.when(gets_if(link))
+        def _():
+            for copy in copies[k]:
+                copy.wait_recv()
+
+    def relay():
+        wait_if(cut, links.index(cut))
+        for link, pair in zip(links, copies):
+            if link[1] == 2:
+
+                @pl.when(sends_if(link))
+                def _(pair=pair):
+                    for copy in pair:
+                        copy.start()
+
+    def first_sends():
+        pl.semaphore_wait(barrier, targets + 10)
+        for link, pair in zip(links, copies):
+            if link[1] == 0:
+
+                @pl.when(sends_if(link))
+                def _(pair=pair):
+                    pair[1].start()
 
     kappa, rho = (
         jnp.concatenate([mat_ref[j, :, y, :] for y in range(ny)], axis=1) for j in range(2)
@@ -274,18 +300,23 @@
         faces_ref[j : j + 1, :] = jnp.concatenate(
             [rows[x : x + 1, (ny - 1) * nz :] for x in range(nx)], axis=1
         )
+        faces_ref[4 + j : 5 + j, :] = jnp.concatenate(
+            [rows[x : x + 1, :nz] for x in range(nx)], axis=1
+        )
         faces_ref[2 + j : 3 + j, :] = jnp.concatenate(
             [rows[nx - 1 :], jnp.zeros((1, width - n), F32)], axis=1
         )
         edge_rows = exact(rows, hot)
         turned = jnp.concatenate([edge_rows, jnp.zeros((128 - nx, 128), F32)], axis=0).T
-        faces_ref[4 + j : 5 + j, :] = jnp.concatenate(
+        fz_ref[j : j + 1, :] = jnp.concatenate(
             [turned[y : y + 1, :nx] for y in range(ny)]
             + [edge_rows[:1, :nx], edge_rows[nx - 1 :, :nx]]
-            + [jnp.zeros((1, width - (ny + 2) * nx), F32)],
+            + [jnp.zeros((1, 256 - (ny + 2) * nx), F32)],
             axis=1,
         )
-    faces_ref[6:8, :] = jnp.zeros((2, width), F32)
+
+    faces_ref[6:, :] = jnp.zeros((2, width), F32)
+    fz_ref[2:, :] = jnp.zeros((6, 256), F32)
 
     def z_edge(x, y, count):
         tall, low = vbuf[x, y, nz - 16 :, :], vbuf[x, y, :16, :]
@@ -293,6 +324,8 @@
         return picked.astype(BF16)
 
     def later_sends():
+        for load in loads[5:]:
+            load.wait()
         for y in range(ny):
             zf_ref[y] = z_edge(slice(None), y, nx)
         zx_ref[...] = jnp.zeros_like(zx_ref)
@@ -300,11 +333,12 @@
             zx_ref[j, :ny] = z_edge(x, slice(None), ny)
         for link, pair in zip(links, copies):
 
-            @pl.when(sends_if(link))
-            def _(link=link, pair=pair):
-                pair[0].start()
-                if link[1]:
-                    pair[1].start()
+            if link[1] < 2:
+
+                @pl.when(sends_if(link))
+                def _(link=link, pair=pair):
+                    for copy in pair if link[1] else pair[:1]:
+                        copy.start()
 
     weights[0].wait()
     starts = np.cumsum([0] + [hi - lo for lo, hi in WINDOWS])
@@ -328,6 +362,8 @@
 
     def load_plane(x):
         if x < nx:
+            if x < 5:
+                loads[x].wait()
             vt[x // 2, :, (x % 2) * n : (x % 2 + 1) * n] = vbuf[x].reshape(n, cols).T
 
     def stage_a(x):
@@ -373,10 +409,9 @@
             acc[1] += part
 
     pairs = nx // 2
-    for load in loads:
-        load.wait()
     for x in range(3):
         stage_a(x)
+    first_sends()
     for i in range(pairs):
         for x in range(2):
             stage_a(2 * i + 3 + x)
@@ -384,15 +419,15 @@
         stage_c(i - 1)
         if i == 0:
             later_sends()
+        if i == RELAY:
+            relay()
     stage_c(pairs - 1)
     for load in weights[1:]:
         load.wait()
 
     for k, link in enumerate(links):
-        @pl.when(gets_if(link))
-        def _(k=k):
-            for copy in copies[k]:
-                copy.wait_recv()
+        if link[1] != 1:
+            wait_if(link, k)
 
     def row(k, r, lo, hi):
         return fh[k, r : r + 1, lo:hi]
@@ -403,61 +438,66 @@
     used = (hx_n + 2) * nz
     blank = jnp.zeros((1, 16), F32)
     edge = (nx - 1) * nz
+
+    later = []
 
     def group(k_at, m_at, halo, kh, rh, own, ko, ro, w_ref, windows):
         k, m = halo.shape[0], own.shape[1]
         ht[:, k_at : k_at + k] = halo.T
         owned[:, m_at : m_at + m] = own
-        kc, rc = (jnp.broadcast_to(r, (128, k)).T for r in (kh, rh))
-        far = jnp.zeros((1, k), F32)
-        first = 0
+        rc = jnp.broadcast_to(rh, (128, k)).T
+        spans = np.cumsum([0] + [hi - lo for lo, hi in windows])
         for t, (lo, hi) in enumerate(windows):
-            tile = w_ref[first : first + hi - lo]
-            first += hi - lo
             lanes = slice(t * 128, (t + 1) * 128)
-            wc, wm = tile[:, :128].astype(F32), tile[:, 128:].astype(F32)
-            ls = (wc * ((-PC) * (kc[lo:hi] + ko[:, lanes]))).astype(BF16)
+            wm = w_ref[spans[t] : spans[t + 1], 128:].astype(F32)
             lm = (wm * (PM * (rc[lo:hi] + ro[:, lanes]))).astype(BF16)
-            fbuf[t, :, :256] = nn(
-                ht[:, k_at + lo : k_at + hi], jnp.concatenate([ls, lm], axis=1)
-            )
-            own_diag = (0.5 * PC) * jnp.sum(wc * kc[lo:hi], axis=0, keepdims=True)
-            part = (0.5 * PC) * exact_nt(ko[:, lanes], tile[:, :128])
-            sides = [jnp.zeros((1, lo), F32), part, jnp.zeros((1, k - hi), F32)]
-            far = far + wide([x for x in sides if x.shape[1]])
             at = slice(m_at + t * 128, m_at + (t + 1) * 128)
-            for r in range(0, cols, 64):
-                rows = slice(r, r + 64)
-                us[rows, at] = (
-                    own_diag * owned[rows, at].astype(F32) + fbuf[t, rows, :128]
-                ).astype(BF16)
-                um[rows, at] = fbuf[t, rows, 128:256].astype(BF16)
-        for r in range(0, cols, 32):
-            rows = slice(r, r + 32)
-            at = slice(k_at, k_at + k)
-            hfar[rows, at] = (far * ht[rows, at].astype(F32)).astype(BF16)
+            um[:, at] = nn(ht[:, k_at + lo : k_at + hi], lm).astype(BF16)
+
+        def stiff():
+            kc = jnp.broadcast_to(kh, (128, k)).T
+            far = jnp.zeros((1, k), F32)
+            for t, (lo, hi) in enumerate(windows):
+                lanes = slice(t * 128, (t + 1) * 128)
+                tile = w_ref[spans[t] : spans[t + 1], :128]
+                wc = tile.astype(F32)
+                ls = (wc * ((-PC) * (kc[lo:hi] + ko[:, lanes]))).astype(BF16)
+                fbuf[t, :, :128] = nn(ht[:, k_at + lo : k_at + hi], ls)
+                own_diag = (0.5 * PC) * jnp.sum(wc * kc[lo:hi], axis=0, keepdims=True)
+                part = (0.5 * PC) * exact_nt(ko[:, lanes], tile)
+                sides = [jnp.zeros((1, lo), F32), part, jnp.zeros((1, k - hi), F32)]
+                far = far + wide([x for x in sides if x.shape[1]])
+                at = slice(m_at + t * 128, m_at + (t + 1) * 128)
+                for r in range(0, cols, 64):
+                    rows = slice(r, r + 64)
+                    us[rows, at] = (
+                        own_diag * owned[rows, at].astype(F32) + fbuf[t, rows, :128]
+                    ).astype(BF16)
+            for r in range(0, cols, 32):
+                rows = slice(r, r + 32)
+                at = slice(k_at, k_at + k)
+                hfar[rows, at] = (far * ht[rows, at].astype(F32)).astype(BF16)
+
+        later.append(stiff)
 
     ky = 2 * 16 + used
-    for side in range(2):
-        if side == 0:
-            pick = lambda r: wide(
-                [blank, row(1, r, edge, edge + nz), row(0, r, 0, used - nz), blank]
-            )
-        else:
-            pick = lambda r: wide(
-                [blank, row(0, r, (hx_n - 1) * nz, nx * nz), row(2, r, 0, nz), blank]
-            )
-        start = side * hx_n
-        none = jnp.zeros((16, cols), BF16)
-        halo = jnp.concatenate(
-            [none, hy[start : start + hx_n + 2].reshape(used, cols), none], axis=0
-        )
-        own = vbuf[start : start + hx_n, 0].reshape(hx_n * nz, cols).T
-        mine = [
-            wide([rows[x : x + 1, :nz] for x in range(start, start + hx_n)])
-            for rows in (kappa, rho)
-        ]
-        group(side * ky, side * n, halo, pick(0), pick(1), own, mine[0], mine[1], wy_ref, YWINDOWS)
+    none = jnp.zeros((16, cols), BF16)
+    lower = lambda r: wide([blank, row(1, r, edge, edge + nz), row(0, r, 0, used - nz), blank])
+    group(
+        0, 0, jnp.concatenate([none, hy[...].reshape(used, cols), none], axis=0),
+        lower(0), lower(1), vbuf[:hx_n, 0].reshape(hx_n * nz, cols).T,
+        *(wide([rows[x : x + 1, :nz] for x in range(hx_n)]) for rows in (kappa, rho)),
+        wy_ref, YWINDOWS,
+    )
+    upper = lambda r: wide(
+        [blank, faces_ref[r : r + 1, (hx_n - 1) * nz :], row(2, r, 0, nz), blank]
+    )
+    mine = vbuf[hx_n - 1 :, ny - 1].reshape(used - nz, cols)
+    group(
+        ky, n, jnp.concatenate([none, mine, hc[...], none], axis=0),
+        upper(0), upper(1), hu[...].reshape(hx_n * nz, cols).T,
+        row(4, 4, hx_n * nz, nx * nz), row(4, 5, hx_n * nz, nx * nz), wy_ref, YWINDOWS,
+    )
 
     group(
         2 * ky, 2 * n, hx[...].reshape(n, cols), row(3, 2, 0, n), row(3, 3, 0, n),
@@ -468,13 +508,12 @@
     low, high = (nf - nx, nf), (0, nx)
 
     def zpick(r):
-        spans = [(4, (0, nf)), (5, low), (6, high), (7, (nf + nx, nf + 2 * nx)),
-                 (8, (nf, nf + nx)), (9, low), (10, high), (11, low), (12, high)]
-        return wide([row(k, r, lo, hi) for k, (lo, hi) in spans])
+        spans = [(0, nf), low, high, (nf + nx, nf + 2 * nx), (nf, nf + nx), low, high, low, high]
+        return wide([fhz[k, r : r + 1, lo:hi] for k, (lo, hi) in enumerate(spans)])
 
     group(
-        2 * ky + n, 3 * n, hz[...].reshape((ny + 8) * nx, cols), zpick(4), zpick(5),
-        zf_ref[...].reshape(nf, cols).T, faces_ref[4:5, :nf], faces_ref[5:6, :nf],
+        2 * ky + n, 3 * n, hz[...].reshape((ny + 8) * nx, cols), zpick(0), zpick(1),
+        zf_ref[...].reshape(nf, cols).T, fz_ref[:1, :nf], fz_ref[1:2, :nf],
         wz_ref, ZWINDOWS,
     )
 
@@ -554,6 +593,8 @@
     symmetrize(1)
     swap(0)
     swap(1)
+    for stiff in later:
+        stiff()
     acc[0] = nt(owned[...], us[...])
     acc[0] += nt(ht[...], hfar[...])
     for pair in range(pairs):
@@ -604,13 +645,13 @@
             pltpu.VMEM((6, cols, 2 * n), F32),
             pltpu.VMEM((2, cols, 2 * n), BF16),
             pltpu.VMEM((2, cols, cols), F32),
-            pltpu.VMEM((nx + 3, nz, cols), BF16),
+            pltpu.VMEM((nx // 2 + 2, nz, cols), BF16),
             pltpu.VMEM((ny, nz, cols), BF16),
             pltpu.VMEM((ny + 8, nx, cols), BF16),
-            pltpu.VMEM((13, 8, width), F32),
+            pltpu.VMEM((5, 8, width), F32),
             pltpu.SemaphoreType.DMA((nx,)),
-            pltpu.SemaphoreType.DMA((26,)),
-            pltpu.SemaphoreType.DMA((26,)),
+            pltpu.SemaphoreType.DMA((29,)),
+            pltpu.SemaphoreType.DMA((29,)),
             pltpu.VMEM((2, 2, 2, 4, 4, 2, 8, cols // 2), F32),
             pltpu.SemaphoreType.DMA((10 * tiles,)),
             pltpu.SemaphoreType.DMA((10 * tiles,)),
@@ -626,6 +667,8 @@
             pltpu.VMEM((cols, halo_cells), BF16),
         ]
         + [pltpu.VMEM((cols, own_cells), BF16)] * 3
+        + [pltpu.VMEM((nx // 2, nz, cols), BF16), pltpu.VMEM((nz, cols), BF16)]
+        + [pltpu.VMEM((2, nx, cols), BF16), pltpu.VMEM((8, 256), F32), pltpu.VMEM((9, 8, 256), F32)]
         + [pltpu.VMEM(x, F32) for row in shapes + keeps for x in row],
         compiler_params=pltpu.CompilerParams(
             collective_id=0, has_side_effects=True, vmem_limit_bytes=63 * 1024 * 1024

time: 61.6 us -> 52.2 us (0.85)
  Pallas kernels: 59.4 us -> 50 us
    pallas_call x1, Pallas kernels: 59.4 us -> 50 us  [local_sums(): pl.pallas_call(kernel, out_shape=jax.ShapeDtypeStruct((8, cols), F32), in...]
where the time goes in v4:
time: 52.2 us; the launch traced here: 52.1 us
  Pallas kernels  50 us (96%)
  local copies, waits for them, and re-layouts  1.4 us (3%)
  between operations  0.64 us (1%)
    pallas_call x1, Pallas kernels, local_sums(): pl.pallas_call(kernel, out_shape=jax.ShapeDtypeStruct((8, cols), F32), in...  50 us
    slice x1, local copies, waits for them, and re-layouts, per_device(): return (both[:4], both[4:])  1.4 us

profile of v4, /device:TPU:0, one launch (start us, length us, event | category | flops | bytes accessed | tf_op | source)
XLA Modules:
  0.0 52.1 jit_solution(3159173165522674742)
XLA Ops:
  0.6 50.0 %local_sums.1 = f32[8,512]{1,0:T(8,128)} custom-call(bf16[16,8,48,512]{3,2,1,0:T(8,128)(2,1)} %refs_0_.1, f32[2,16,8,48]{3,2,1,0:T(8,128)} %refs_1_.1, bf16[896,256]{1,0:T(8,128)(2,1)} %constant.6.clone.refs_2_, bf16[768,256]{1,0:T(8,128)(2,1)} %constant.7.clone.refs_3_, bf16[256,256]{1,0:T(8,128)(2,1)} %constant.8.clone.refs_4_), custom_call_target="tpu_custom_call" | custom-call | tf_op jit(solution)/shard_map/local_sums/pallas_call | solution.py:637
  50.7 1.4 %fusion = (f32[4,512]{1,0:T(4,128)}, f32[4,512]{1,0:T(4,128)}) fusion(f32[8,512]{1,0:T(8,128)} %local_sums.1), kind=kLoop, calls=%fused_computation | loop fusion | bytes 32768 | tf_op jit(solution)/shard_map/slice | solution.py:682

commit v5 on v4

--- a/solution.py
+++ b/solution.py
@@ -287,6 +287,7 @@
                 def _(pair=pair):
                     pair[1].start()
 
+    first_sends()
     kappa, rho = (
         jnp.concatenate([mat_ref[j, :, y, :] for y in range(ny)], axis=1) for j in range(2)
     )
@@ -411,7 +412,6 @@
     pairs = nx // 2
     for x in range(3):
         stage_a(x)
-    first_sends()
     for i in range(pairs):
         for x in range(2):
             stage_a(2 * i + 3 + x)
@@ -636,7 +636,7 @@
     )
     return pl.pallas_call(
         kernel,
-        out_shape=jax.ShapeDtypeStruct((8, cols), F32),
+        out_shape=pltpu.VMEM((8, cols), F32),
         in_specs=[anyspace, vmem] + [anyspace] * 3,
         out_specs=vmem,
         scratch_shapes=[

time: 52.2 us -> 49.7 us (0.952)
  Pallas kernels: 50 us -> 48.4 us
  local copies, waits for them, and re-layouts: 1.4 us -> 0.61 us
    pallas_call x1, Pallas kernels: 50 us -> 48.4 us  [local_sums(): pl.pallas_call(kernel, out_shape=pltpu.VMEM((8, cols), F32), in_specs=[an...]
    slice x1, local copies, waits for them, and re-layouts: 1.4 us -> 0.61 us  [per_device(): return (both[:4], both[4:])]
where the time goes in v5:
time: 49.7 us; the launch traced here: 49.6 us
  Pallas kernels  48.4 us (97%)
  between operations  0.64 us (1%)
  local copies, waits for them, and re-layouts  0.61 us (1%)
    pallas_call x1, Pallas kernels, local_sums(): pl.pallas_call(kernel, out_shape=pltpu.VMEM((8, cols), F32), in_specs=[an...  48.4 us

profile of v5, /device:TPU:0, one launch (start us, length us, event | category | flops | bytes accessed | tf_op | source)
XLA Modules:
  0.0 49.6 jit_solution(3929714775695839948)
XLA Ops:
  0.6 48.4 %local_sums.1 = f32[8,512]{1,0:T(8,128)S(1)} custom-call(bf16[16,8,48,512]{3,2,1,0:T(8,128)(2,1)} %refs_0_.1, f32[2,16,8,48]{3,2,1,0:T(8,128)} %refs_1_.1, bf16[896,256]{1,0:T(8,128)(2,1)} %constant.6.clone.refs_2_, bf16[768,256]{1,0:T(8,128)(2,1)} %constant.7.clone.refs_3_, bf16[256,256]{1,0:T(8,128)(2,1)} %constant.8.clone.refs_4_), custom_call_target="tpu_custom_call" | custom-call | tf_op jit(solution)/shard_map/local_sums/pallas_call | solution.py:637
  49.0 0.6 %fusion = (f32[4,512]{1,0:T(4,128)}, f32[4,512]{1,0:T(4,128)}) fusion(f32[8,512]{1,0:T(8,128)S(1)} %local_sums.1), kind=kLoop, calls=%fused_computation | loop fusion | bytes 32768 | tf_op jit(solution)/shard_map/slice | solution.py:682

commit v6 on v5

--- a/solution.py
+++ b/solution.py
@@ -39,6 +39,7 @@
 
 
 RELAY = 5
+EARLY = 4
 
 
 def banded(w, windows):
@@ -425,9 +426,9 @@
     for load in weights[1:]:
         load.wait()
 
-    for k, link in enumerate(links):
-        if link[1] != 1:
-            wait_if(link, k)
+    def wait_for(*ks):
+        for k in ks:
+            wait_if(links[k], k)
 
     def row(k, r, lo, hi):
         return fh[k, r : r + 1, lo:hi]
@@ -481,6 +482,30 @@
         later.append(stiff)
 
     ky = 2 * 16 + used
+    acc[0] = nt(vt[0], ys[0])
+    for pair in range(1, EARLY):
+        acc[0] += nt(vt[pair], ys[pair])
+    wait_for(3)
+    group(
+        2 * ky, 2 * n, hx[...].reshape(n, cols), row(3, 2, 0, n), row(3, 3, 0, n),
+        vt[0, :, :n], kappa[:1], rho[:1], wp_ref, WINDOWS,
+    )
+
+    wait_for(*range(6, 14))
+    nf = nx * ny
+    low, high = (nf - nx, nf), (0, nx)
+
+    def zpick(r):
+        spans = [(0, nf), low, high, (nf + nx, nf + 2 * nx), (nf, nf + nx), low, high, low, high]
+        return wide([fhz[k, r : r + 1, lo:hi] for k, (lo, hi) in enumerate(spans)])
+
+    group(
+        2 * ky + n, 3 * n, hz[...].reshape((ny + 8) * nx, cols), zpick(0), zpick(1),
+        zf_ref[...].reshape(nf, cols).T, fz_ref[:1, :nf], fz_ref[1:2, :nf],
+        wz_ref, ZWINDOWS,
+    )
+
+    wait_for(0, 1)
     none = jnp.zeros((16, cols), BF16)
     lower = lambda r: wide([blank, row(1, r, edge, edge + nz), row(0, r, 0, used - nz), blank])
     group(
@@ -489,6 +514,7 @@
         *(wide([rows[x : x + 1, :nz] for x in range(hx_n)]) for rows in (kappa, rho)),
         wy_ref, YWINDOWS,
     )
+    wait_for(2, 4)
     upper = lambda r: wide(
         [blank, faces_ref[r : r + 1, (hx_n - 1) * nz :], row(2, r, 0, nz), blank]
     )
@@ -497,24 +523,6 @@
         ky, n, jnp.concatenate([none, mine, hc[...], none], axis=0),
         upper(0), upper(1), hu[...].reshape(hx_n * nz, cols).T,
         row(4, 4, hx_n * nz, nx * nz), row(4, 5, hx_n * nz, nx * nz), wy_ref, YWINDOWS,
-    )
-
-    group(
-        2 * ky, 2 * n, hx[...].reshape(n, cols), row(3, 2, 0, n), row(3, 3, 0, n),
-        vt[0, :, :n], kappa[:1], rho[:1], wp_ref, WINDOWS,
-    )
-
-    nf = nx * ny
-    low, high = (nf - nx, nf), (0, nx)
-
-    def zpick(r):
-        spans = [(0, nf), low, high, (nf + nx, nf + 2 * nx), (nf, nf + nx), low, high, low, high]
-        return wide([fhz[k, r : r + 1, lo:hi] for k, (lo, hi) in enumerate(spans)])
-
-    group(
-        2 * ky + n, 3 * n, hz[...].reshape((ny + 8) * nx, cols), zpick(0), zpick(1),
-        zf_ref[...].reshape(nf, cols).T, fz_ref[:1, :nf], fz_ref[1:2, :nf],
-        wz_ref, ZWINDOWS,
     )
 
     core, zl = lax.rem(gx, 2), gx // 2
@@ -595,11 +603,11 @@
     swap(1)
     for stiff in later:
         stiff()
-    acc[0] = nt(owned[...], us[...])
+    acc[0] += nt(owned[...], us[...])
     acc[0] += nt(ht[...], hfar[...])
-    for pair in range(pairs):
+    for pair in range(EARLY, pairs):
         acc[0] += nt(vt[pair], ys[pair])
-        if pair == 1:
+        if pair == 6:
             swapped(0)
             swapped(1)
     symmetrize(0)

time: 49.7 us -> 48.9 us (0.984)
  Pallas kernels: 48.4 us -> 47.5 us
    pallas_call x1, Pallas kernels: 48.4 us -> 47.5 us  [local_sums(): pl.pallas_call(kernel, out_shape=pltpu.VMEM((8, cols), F32), in_specs=[an...]
where the time goes in v6:
time: 48.9 us; the launch traced here: 48.8 us
  Pallas kernels  47.5 us (97%)
  between operations  0.64 us (1%)
  local copies, waits for them, and re-layouts  0.61 us (1%)
    pallas_call x1, Pallas kernels, local_sums(): pl.pallas_call(kernel, out_shape=pltpu.VMEM((8, cols), F32), in_specs=[an...  47.5 us

profile of v6, /device:TPU:0, one launch (start us, length us, event | category | flops | bytes accessed | tf_op | source)
XLA Modules:
  0.0 48.8 jit_solution(17561501715622242731)
XLA Ops:
  0.6 47.5 %local_sums.1 = f32[8,512]{1,0:T(8,128)S(1)} custom-call(bf16[16,8,48,512]{3,2,1,0:T(8,128)(2,1)} %refs_0_.1, f32[2,16,8,48]{3,2,1,0:T(8,128)} %refs_1_.1, bf16[896,256]{1,0:T(8,128)(2,1)} %constant.6.clone.refs_2_, bf16[768,256]{1,0:T(8,128)(2,1)} %constant.7.clone.refs_3_, bf16[256,256]{1,0:T(8,128)(2,1)} %constant.8.clone.refs_4_), custom_call_target="tpu_custom_call" | custom-call | tf_op jit(solution)/shard_map/local_sums/pallas_call | solution.py:645
  48.2 0.6 %fusion = (f32[4,512]{1,0:T(4,128)}, f32[4,512]{1,0:T(4,128)}) fusion(f32[8,512]{1,0:T(8,128)S(1)} %local_sums.1), kind=kLoop, calls=%fused_computation | loop fusion | bytes 32768 | tf_op jit(solution)/shard_map/slice | solution.py:690

commit v7 on v6

--- a/solution.py
+++ b/solution.py
@@ -110,7 +110,7 @@
     return joined(nt(split(a), b), a.shape[0])
 
 
-ORDERS = ("yxz", "xzy", "zyx", "xyz")
+ORDERS = ("zyx", "zxy", "yxz", "xyz")
 GONE = {"x": "x", "y": "y", "z": "lh"}
 SIZE = {"l": 2, "h": 2, "x": 4, "y": 4}
 tiles = len(ORDERS)

time: 48.9 us -> 48.7 us (level)
  no operation moved by 1% of the time
where the time goes in v7:
time: 48.7 us; the launch traced here: 48.6 us
  Pallas kernels  47.3 us (97%)
  between operations  0.64 us (1%)
  local copies, waits for them, and re-layouts  0.61 us (1%)
    pallas_call x1, Pallas kernels, local_sums(): pl.pallas_call(kernel, out_shape=pltpu.VMEM((8, cols), F32), in_specs=[an...  47.3 us

profile of v7, /device:TPU:0, one launch (start us, length us, event | category | flops | bytes accessed | tf_op | source)
XLA Modules:
  0.0 48.6 jit_solution(7090124015950085477)
XLA Ops:
  0.6 47.3 %local_sums.1 = f32[8,512]{1,0:T(8,128)S(1)} custom-call(bf16[16,8,48,512]{3,2,1,0:T(8,128)(2,1)} %refs_0_.1, f32[2,16,8,48]{3,2,1,0:T(8,128)} %refs_1_.1, bf16[896,256]{1,0:T(8,128)(2,1)} %constant.6.clone.refs_2_, bf16[768,256]{1,0:T(8,128)(2,1)} %constant.7.clone.refs_3_, bf16[256,256]{1,0:T(8,128)(2,1)} %constant.8.clone.refs_4_), custom_call_target="tpu_custom_call" | custom-call | tf_op jit(solution)/shard_map/local_sums/pallas_call | solution.py:645
  48.0 0.6 %fusion = (f32[4,512]{1,0:T(4,128)}, f32[4,512]{1,0:T(4,128)}) fusion(f32[8,512]{1,0:T(8,128)S(1)} %local_sums.1), kind=kLoop, calls=%fused_computation | loop fusion | bytes 32768 | tf_op jit(solution)/shard_map/slice | solution.py:690
